TPU v7x, 32 devices: a whole 2x2x4 slice. The times are simulated.
32 devices in a mesh: dp: 8 (over z, x), feat: 4 (over y, core).
Axes of the slice: x: 2, y: 2, z: 4, core: 2. Of those that a mesh axis runs over, the one named last changes fastest.
Arguments:
- tokens: bfloat16 [8192, 768], P(('dp', 'feat')), may hold values from -11 to 11
- lengths: int32 [8, 2], replicated, may hold values from 0 to 1024, as said below
- joint_weight: bfloat16 [768, 2304], replicated, may hold values from -0.21875 to 0.21875
- joint_bias: float32 [2304], replicated, may hold values from -17.5 to 17.5
- output_weight: bfloat16 [768, 768], replicated, may hold values from -1.75 to 1.75
- output_bias: float32 [768], replicated, may hold values from -2.4 to 2.4
- first_gain: float32 [768], replicated, may hold values from 0.5 to 1.5
- first_shift: float32 [768], replicated, may hold values from -1 to 1
- up_weight: bfloat16 [768, 3072], replicated, may hold values from -0.21875 to 0.21875
- up_bias: float32 [3072], replicated, may hold values from -1 to 1
- down_weight: bfloat16 [3072, 768], replicated, may hold values from -0.109375 to 0.109375
- down_bias: float32 [768], replicated, may hold values from -1 to 1
- second_gain: float32 [768], replicated, may hold values from 0.5 to 1.5
- second_shift: float32 [768], replicated, may hold values from -1 to 1
- feature_matrix: bfloat16 [12, 256, 64], P(None, 'feat'), may hold values from -6 to 6
- cotangent: bfloat16 [8192, 768], P(('dp', 'feat')), may hold values from -6 to 6
Outputs:
- layer_output: bfloat16 [8192, 768], P(('dp', 'feat'))
- input_gradient: float32 [8192, 768], P(('dp', 'feat'))
- grad_joint: float32 [768, 2304], P(('dp', 'feat'))
- grad_jointbias: float32 [2304], P(('dp', 'feat'))
- grad_output: float32 [768, 768], P(('dp', 'feat'))
- grad_outputbias: float32 [768], P(('dp', 'feat'))
- grad_firstgain: float32 [768], P(('dp', 'feat'))
- grad_firstshift: float32 [768], P(('dp', 'feat'))
- grad_up: float32 [768, 3072], P(('dp', 'feat'))
- grad_upbias: float32 [3072], P(('dp', 'feat'))
- grad_down: float32 [3072, 768], P(('dp', 'feat'))
- grad_downbias: float32 [768], P(('dp', 'feat'))
- grad_secondgain: float32 [768], P(('dp', 'feat'))
- grad_secondshift: float32 [768], P(('dp', 'feat'))
- token_moments: float32 [3], replicated
Inputs may be any that keep to these rules, and one draw needn't show every extreme that they name: In each row the nonzero lengths come first, each 1024 or more, and they add up to at most 1024; some row holds one sequence of 1024 tokens.
All inputs are finite; a program needn't handle non-finite values.
Results may differ from a plain program's by a relative error of at most 0.035.
Values may be sent and summed in bfloat16 or wider, within the bound.
A program may use at most 192 MiB of HBM per device.

v0:
```python
import jax
import jax.numpy as jnp
from jax import lax
from jax.sharding import PartitionSpec as P

epsilon = 1e-06


def layer_norm(residual, scaling, offset):
    center = residual - jnp.mean(residual, -1, keepdims=True)
    spread = jnp.mean(center * center, -1, keepdims=True)
    return center * lax.rsqrt(spread + epsilon) * scaling + offset


def exact_gelu(input_value_rows):
    return jax.nn.gelu(input_value_rows, approximate=False)


def feature_logits(
    joint_rows, random_feature_rows, score_scale_factor, model_width, head_count, head_size
):
    row_count = joint_rows.shape[0]
    query_matrix = joint_rows[:, :model_width].reshape(row_count, head_count, head_size)
    input_key_rows = joint_rows[:, model_width : 2 * model_width].reshape(
        row_count, head_count, head_size
    )
    input_value_rows = joint_rows[:, 2 * model_width :].reshape(row_count, head_count, head_size)
    queries_wide = query_matrix.astype(jnp.float32)
    keys_wide = input_key_rows.astype(jnp.float32)
    query_feature_scores = score_scale_factor * jnp.einsum(
        "bjv,jsv->bjs", query_matrix, random_feature_rows, preferred_element_type=jnp.float32
    )
    key_feature_scores = score_scale_factor * jnp.einsum(
        "bjv,jsv->bjs", input_key_rows, random_feature_rows, preferred_element_type=jnp.float32
    )
    query_sq = (
        score_scale_factor * score_scale_factor * jnp.sum(queries_wide * queries_wide, -1) / 2
    )
    key_sq = score_scale_factor * score_scale_factor * jnp.sum(keys_wide * keys_wide, -1) / 2
    return (
        input_value_rows,
        queries_wide,
        keys_wide,
        query_feature_scores - query_sq[..., None],
        key_feature_scores - key_sq[..., None],
    )


def segment_state(key_feats, input_value_rows, member_low):
    padded_key_rows = key_feats * member_low[:, None, None]
    state_part = jnp.einsum(
        "isu,isn->sun", padded_key_rows, input_value_rows, preferred_element_type=jnp.float32
    )
    return (state_part, jnp.sum(padded_key_rows, axis=0, dtype=jnp.float32))


def apply_state(query_feature_maps, member_low, sequence_key_state, totals):
    padded_query_rows = query_feature_maps * member_low[:, None, None]
    numer_part = jnp.einsum(
        "rif,ifw->riw", padded_query_rows, sequence_key_state, preferred_element_type=jnp.float32
    )
    denom_part = jnp.einsum(
        "thm,hm->th", padded_query_rows.astype(jnp.float32), totals, precision=lax.Precision.HIGHEST
    )
    return (numer_part, denom_part)


def query_feature_grad(numerator_segment, denom_seg, sequence_key_state, totals):
    first_term = jnp.einsum(
        "bjv,jsv->bjs", numerator_segment, sequence_key_state, preferred_element_type=jnp.float32
    )
    return first_term + jnp.einsum(
        "th,hm->thm", denom_seg.astype(jnp.float32), totals, precision=lax.Precision.HIGHEST
    )


def state_grad_terms(query_feature_maps, numerator_segment, denom_seg):
    state_part = jnp.einsum(
        "isu,isn->sun", query_feature_maps, numerator_segment, preferred_element_type=jnp.float32
    )
    totals_part = jnp.einsum(
        "thm,th->hm", query_feature_maps, denom_seg, preferred_element_type=jnp.float32
    )
    return (state_part, totals_part)


def key_value_grad(input_value_rows, key_feats, member_low, state_gradient_terms, totals_grad):
    key_part = (
        jnp.einsum(
            "bjv,jsv->bjs",
            input_value_rows,
            state_gradient_terms,
            preferred_element_type=jnp.float32,
        )
        + totals_grad[None]
    )
    key_part = member_low.astype(jnp.float32)[:, None, None] * key_part
    value_part = jnp.einsum(
        "rif,ifw->riw",
        key_feats * member_low[:, None, None],
        state_gradient_terms,
        preferred_element_type=jnp.float32,
    )
    return (key_part, value_part)


def logit_to_input(feature_back, raw_feats, random_feature_rows, inputs_wide, score_scale_factor):
    logit_grad = feature_back * raw_feats
    linear_part = score_scale_factor * jnp.einsum(
        "rif,ifw->riw",
        logit_grad.astype(jnp.bfloat16),
        random_feature_rows,
        preferred_element_type=jnp.float32,
    )
    return (
        linear_part
        - score_scale_factor * score_scale_factor * inputs_wide * jnp.sum(logit_grad, -1)[..., None]
    )


def on_device(
    tokens,
    lengths,
    joint_weight,
    joint_bias,
    output_weight,
    output_bias,
    first_gain,
    first_shift,
    up_weight,
    up_bias,
    down_weight,
    down_bias,
    second_gain,
    second_shift,
    feature_matrix,
    cotangent,
):
    local_rows = tokens.shape[0]
    group_size = lax.axis_size("feat")
    row_length = local_rows * group_size
    model_width = tokens.shape[1]
    head_count = feature_matrix.shape[0]
    feature_total = feature_matrix.shape[1] * group_size
    head_size = feature_matrix.shape[2]
    score_scale_factor = head_size ** (-0.25)
    feature_norm = feature_total ** (-0.5)
    slot_count = lengths.shape[1]
    row_lengths = lax.dynamic_index_in_dim(lengths, lax.axis_index("dp"), 0, keepdims=False)
    seq_ends = jnp.cumsum(row_lengths)
    positions = jnp.arange(row_length, dtype=jnp.int32)
    segment_row = jnp.sum((positions[:, None] >= seq_ends[None, :]).astype(jnp.int32), axis=1)
    valid_row = (positions < seq_ends[slot_count - 1]).astype(jnp.float32)
    own_start = lax.axis_index("feat") * local_rows
    valid_own = lax.dynamic_slice_in_dim(valid_row, own_start, local_rows)
    joint_local = (
        jnp.dot(tokens, joint_weight, preferred_element_type=jnp.float32) + joint_bias
    ).astype(jnp.bfloat16)
    joint_rows = lax.all_gather(joint_local, "feat", axis=0, tiled=True)
    input_value_rows, queries_wide, keys_wide, query_shift, key_shift = feature_logits(
        joint_rows, feature_matrix, score_scale_factor, model_width, head_count, head_size
    )
    query_top, key_top = (
        lax.pmax(jnp.max(query_shift, -1).astype(jnp.bfloat16), "feat").astype(jnp.float32),
        lax.pmax(
            jnp.max(jnp.where(valid_row[:, None, None] > 0, key_shift, -1e30), axis=(0, 2)).astype(
                jnp.bfloat16
            ),
            "feat",
        ).astype(jnp.float32),
    )
    member_masks = [(segment_row == segment).astype(jnp.bfloat16) for segment in range(slot_count)]
    query_raw = jnp.exp(query_shift - query_top[..., None]) * feature_norm
    key_raw = jnp.exp(key_shift - key_top[None, :, None]) * feature_norm * valid_row[:, None, None]
    query_feature_maps = query_raw.astype(jnp.bfloat16)
    key_feats = key_raw.astype(jnp.bfloat16)
    numerator = jnp.zeros((row_length, head_count, head_size), jnp.float32)
    denominator = jnp.zeros((row_length, head_count), jnp.float32)
    seq_states = []
    seq_totals = []
    for segment in range(slot_count):
        state_part, totals = segment_state(key_feats, input_value_rows, member_masks[segment])
        sequence_key_state = state_part.astype(jnp.bfloat16)
        numer_part, denom_part = apply_state(
            query_feature_maps, member_masks[segment], sequence_key_state, totals
        )
        numerator = numerator + numer_part
        denominator = denominator + denom_part
        seq_states.append(sequence_key_state)
        seq_totals.append(totals)
    numer_own, denom_own = (
        lax.psum_scatter(
            numerator.reshape(row_length, model_width).astype(jnp.bfloat16),
            "feat",
            scatter_dimension=0,
            tiled=True,
        ).astype(jnp.float32),
        lax.psum_scatter(
            denominator.astype(jnp.bfloat16), "feat", scatter_dimension=0, tiled=True
        ).astype(jnp.float32),
    )
    safe_denom = denom_own + (1.0 - valid_own)[:, None]
    numer_cube = numer_own.reshape(local_rows, head_count, head_size)
    attention = (
        (numer_cube / safe_denom[..., None]).astype(jnp.bfloat16).reshape(local_rows, model_width)
    )
    branch_attn = (
        jnp.dot(attention, output_weight, preferred_element_type=jnp.float32) + output_bias
    )
    tokens_wide = tokens.astype(jnp.float32)
    first_sum = tokens_wide + branch_attn
    hidden, first_pull = jax.vjp(layer_norm, first_sum, first_gain, first_shift)
    hidden_low = hidden.astype(jnp.bfloat16)
    pre_act = jnp.dot(hidden_low, up_weight, preferred_element_type=jnp.float32) + up_bias
    gelu_value, gelu_pull = jax.vjp(exact_gelu, pre_act)
    activated = gelu_value.astype(jnp.bfloat16)
    branch_ffn = jnp.dot(activated, down_weight, preferred_element_type=jnp.float32) + down_bias
    second_sum = hidden + branch_ffn
    normed, second_pull = jax.vjp(layer_norm, second_sum, second_gain, second_shift)
    layer_output = (normed * valid_own[:, None]).astype(jnp.bfloat16)
    moments = jnp.stack(
        [
            jnp.sum(valid_own * jnp.sum(tokens_wide * tokens_wide, -1)),
            jnp.sum(valid_own * jnp.sum(branch_attn * branch_attn, -1)),
            jnp.sum(valid_own * jnp.sum(branch_ffn * branch_ffn, -1)),
        ]
    )
    moment_sums = lax.psum(moments, ("dp", "feat"))
    valid_count = jnp.sum(lengths).astype(jnp.float32)
    token_moments = jnp.sqrt(moment_sums / (valid_count * model_width))
    out_grad = cotangent.astype(jnp.float32) * valid_own[:, None]
    second_grad, grad_secondgain, grad_secondshift = second_pull(out_grad)
    ffn_low = second_grad.astype(jnp.bfloat16)
    grad_down = jnp.einsum("tf,td->fd", activated, ffn_low, preferred_element_type=jnp.float32)
    grad_downbias = jnp.sum(ffn_low.astype(jnp.float32), 0)
    act_grad = jnp.einsum("td,fd->tf", ffn_low, down_weight, preferred_element_type=jnp.float32)
    pre_grad = gelu_pull(act_grad)[0]
    pre_low = pre_grad.astype(jnp.bfloat16)
    grad_up = jnp.einsum("td,tf->df", hidden_low, pre_low, preferred_element_type=jnp.float32)
    grad_upbias = jnp.sum(pre_low.astype(jnp.float32), 0)
    hidden_grad = second_grad + jnp.einsum(
        "tf,df->td", pre_low, up_weight, preferred_element_type=jnp.float32
    )
    first_grad, grad_firstgain, grad_firstshift = first_pull(hidden_grad)
    branch_low = first_grad.astype(jnp.bfloat16)
    grad_output = jnp.einsum("td,te->de", attention, branch_low, preferred_element_type=jnp.float32)
    grad_outputbias = jnp.sum(branch_low.astype(jnp.float32), 0)
    ratio_grad = jnp.einsum(
        "te,de->td", branch_low, output_weight, preferred_element_type=jnp.float32
    ).reshape(local_rows, head_count, head_size)
    numer_grad = (ratio_grad / safe_denom[..., None]).astype(jnp.bfloat16)
    denom_grad = (-jnp.sum(ratio_grad * numer_cube / jnp.square(safe_denom)[..., None], -1)).astype(
        jnp.bfloat16
    )
    numer_back, denom_back = (
        lax.all_gather(numer_grad.reshape(local_rows, model_width), "feat", axis=0, tiled=True),
        lax.all_gather(denom_grad, "feat", axis=0, tiled=True),
    )
    numer_back = numer_back.reshape(row_length, head_count, head_size)
    query_back = jnp.zeros(query_raw.shape, jnp.float32)
    key_back = jnp.zeros(key_raw.shape, jnp.float32)
    value_back = jnp.zeros((row_length, head_count, head_size), jnp.float32)
    for segment in range(slot_count):
        member_low = member_masks[segment]
        numerator_segment = numer_back * member_low[:, None, None]
        denom_seg = denom_back * member_low[:, None]
        query_back = query_back + query_feature_grad(
            numerator_segment, denom_seg, seq_states[segment], seq_totals[segment]
        )
        state_part, totals_grad = state_grad_terms(query_feature_maps, numerator_segment, denom_seg)
        key_part, value_part = key_value_grad(
            input_value_rows, key_feats, member_low, state_part.astype(jnp.bfloat16), totals_grad
        )
        key_back = key_back + key_part
        value_back = value_back + value_part
    query_grad = logit_to_input(
        query_back, query_raw, feature_matrix, queries_wide, score_scale_factor
    )
    key_grad = logit_to_input(key_back, key_raw, feature_matrix, keys_wide, score_scale_factor)
    joint_back = jnp.concatenate(
        [
            query_grad.reshape(row_length, model_width),
            key_grad.reshape(row_length, model_width),
            value_back.reshape(row_length, model_width),
        ],
        axis=1,
    )
    joint_grad = lax.psum_scatter(
        joint_back.astype(jnp.bfloat16), "feat", scatter_dimension=0, tiled=True
    )
    grad_joint = jnp.einsum("td,te->de", tokens, joint_grad, preferred_element_type=jnp.float32)
    grad_jointbias = jnp.sum(joint_grad.astype(jnp.float32), 0)
    input_gradient = first_grad + jnp.einsum(
        "te,de->td", joint_grad, joint_weight, preferred_element_type=jnp.float32
    )
    summed = (
        lax.psum_scatter(grad_joint, ("dp", "feat"), scatter_dimension=0, tiled=True),
        lax.psum_scatter(grad_jointbias, ("dp", "feat"), scatter_dimension=0, tiled=True),
        lax.psum_scatter(grad_output, ("dp", "feat"), scatter_dimension=0, tiled=True),
        lax.psum_scatter(grad_outputbias, ("dp", "feat"), scatter_dimension=0, tiled=True),
        lax.psum_scatter(grad_firstgain, ("dp", "feat"), scatter_dimension=0, tiled=True),
        lax.psum_scatter(grad_firstshift, ("dp", "feat"), scatter_dimension=0, tiled=True),
        lax.psum_scatter(grad_up, ("dp", "feat"), scatter_dimension=0, tiled=True),
        lax.psum_scatter(grad_upbias, ("dp", "feat"), scatter_dimension=0, tiled=True),
        lax.psum_scatter(grad_down, ("dp", "feat"), scatter_dimension=0, tiled=True),
        lax.psum_scatter(grad_downbias, ("dp", "feat"), scatter_dimension=0, tiled=True),
        lax.psum_scatter(grad_secondgain, ("dp", "feat"), scatter_dimension=0, tiled=True),
        lax.psum_scatter(grad_secondshift, ("dp", "feat"), scatter_dimension=0, tiled=True),
    )
    return (
        layer_output,
        input_gradient,
        summed[0],
        summed[1],
        summed[2],
        summed[3],
        summed[4],
        summed[5],
        summed[6],
        summed[7],
        summed[8],
        summed[9],
        summed[10],
        summed[11],
        token_moments,
    )


def solution(mesh):
    in_specs = (
        P(("dp", "feat"), None),
        P(),
        P(),
        P(),
        P(),
        P(),
        P(),
        P(),
        P(),
        P(),
        P(),
        P(),
        P(),
        P(),
        P(None, "feat", None),
        P(("dp", "feat"), None),
    )
    out_specs = (
        P(("dp", "feat"), None),
        P(("dp", "feat"), None),
        P(("dp", "feat"), None),
        P(("dp", "feat")),
        P(("dp", "feat"), None),
        P(("dp", "feat")),
        P(("dp", "feat")),
        P(("dp", "feat")),
        P(("dp", "feat"), None),
        P(("dp", "feat")),
        P(("dp", "feat"), None),
        P(("dp", "feat")),
        P(("dp", "feat")),
        P(("dp", "feat")),
        P(),
    )
    return jax.shard_map(
        on_device, mesh=mesh, in_specs=in_specs, out_specs=out_specs, check_vma=False
    )
```

profile of v0, /device:TPU:0, one launch (start us, length us, event | category | flops | bytes accessed | tf_op | source)
XLA Modules:
  0.0 787.3 jit_solution(4421540872330110038)
XLA Ops:
  7.3 1.9 copy-done
  9.2 3.1 fusion
  15.9 36.7 %all-gather.3.cloned.1.call-done = bf16[1024,2304]{1,0:T(8,128)(2,1)} async-done(((bf16[256,2304]{1,0:T(8,128)(2,1)}), bf16[1024,2304]{1,0:T(8,128)(2,1)}) %all-gather.3.cloned.1.call-update) | async-done | bytes 4718608 | tf_op jit(solution)/shard_map/all_gather | solution.py:159
  52.7 4.6 fusion.98
  57.3 2.6 copy.79
  59.9 2.6 copy.80
  62.5 1.8 fusion.4
  65.0 2.7 copy.78
  67.6 1.9 fusion.1
  69.6 4.3 fusion.13
  74.0 2.9 select_reduce_fusion
  76.9 11.8 %all-reduce.9 = (bf16[1024,12]{0,1:T(8,128)(2,1)}, bf16[12]{0:T(256)(128)(2,1)}) all-reduce(bf16[1024,12]{0,1:T(8,128)(2,1)} %get-tuple-element.139, bf16[12]{0:T(256)(128)(2,1)} %get-tuple-element.141), channel_id=1, replica_groups=mesh['dp'=8,'feat'=4] {'feat'}, use_global_device_ids=true, to_apply=%region_7.8 | all-reduce | flops 12300 | bytes 49200 | tf_op jit(solution)/shard_map/pmax | solution.py:164
  89.4 3.2 convert_reduce_fusion.2
  98.5 2.2 fusion.30
  100.8 1.8 add_convert_fusion.2
  102.6 2.6 copy.83
  105.9 13.4 %reduce-scatter.12.cloned.1.call-done = bf16[256,12]{0,1:T(8,128)(2,1)} async-done(((bf16[1024,12]{0,1:T(8,128)(2,1)}), bf16[256,12]{0,1:T(8,128)(2,1)}) %reduce-scatter.12.cloned.1.call-update) | async-done | bytes 6160 | tf_op jit(solution)/shard_map/reduce_scatter | solution.py:198
  121.5 2.3 copy.84
  123.8 26.0 %reduce-scatter.10.cloned.1.call-done = bf16[256,768]{1,0:T(8,128)(2,1)} async-done(((bf16[1024,768]{1,0:T(8,128)(2,1)}), bf16[256,768]{1,0:T(8,128)(2,1)}) %reduce-scatter.10.cloned.1.call-update) | async-done | bytes 393232 | tf_op jit(solution)/shard_map/reduce_scatter | solution.py:192
  149.8 3.1 fusion.96
  153.3 9.9 %multiply_convert_fusion = (bf16[256,3072]{1,0:T(8,128)(2,1)S(1)}, f32[256,3072]{1,0:T(8,128)S(1)}, f32[256,3072]{1,0:T(8,128)S(1)}) fusion(f32[3072]{0:T(1024)S(1)} %copy-done.67, bf16[768,3072]{1,0:T(8,128)(2,1)} %param.24, f32[256,768]{1,0:T(8,128)S(1)} %get-tuple-element.116, f32[768]{0:T(1024)S(1)} %copy-done.36, f32[768]{0:T(1024)S(1)} %copy-done.35, ...), kind=kOutput, calls=%fused_computation.24 | convolution fusion | flops 1260847104 | bytes 13389824 | tf_op jit(solution)/shard_map/dot_general | solution.py:214
  163.3 2.2 fusion.93
  168.7 2.7 convert_reduce_fusion
  171.4 2.3 multiply_reduce_fusion.3
  177.4 2.3 copy.87
  180.9 5.4 all_gather.11
  187.0 1.9 fusion.72
  189.5 1.9 fusion.70
  192.0 5.1 all-gather.5.cloned.1.call-done
  197.1 2.6 copy.86
  199.8 2.6 fusion.45
  207.9 1.9 fusion.100
  211.8 1.9 fusion.99
  215.9 2.5 pad_maximum_fusion
  218.5 3.3 fusion.86
  221.9 7.9 %fusion.83 = f32[768,3072]{1,0:T(8,128)} fusion(bf16[256,3072]{1,0:T(8,128)(2,1)} %copy-done.23, f32[256,768]{1,0:T(8,128)} %copy-done.12, f32[768]{0:T(1024)S(1)} %copy-done.36, f32[768]{0:T(1024)S(1)} %copy-done.35, f32[256]{0:T(256)S(1)} %copy-done.53, f32[256]{0:T(256)S(1)} %copy-done.41), kind=kOutput, calls=%fused_computation.167 | convolution fusion | flops 1208942592 | bytes 11804672 | tf_op jit(solution)/shard_map/td,tf->df/dot_general | solution.py:239
  229.8 6.6 fusion.102
  236.8 29.6 %reduce-scatter.14.cloned.1.call-done = bf16[256,2304]{0,1:T(8,128)(2,1)} async-done(((bf16[1024,2304]{0,1:T(8,128)(2,1)}), bf16[256,2304]{0,1:T(8,128)(2,1)}) %reduce-scatter.14.cloned.1.call-update) | async-done | bytes 1179664 | tf_op jit(solution)/shard_map/reduce_scatter | solution.py:288
  266.4 5.3 convolution_bitcast_fusion
  271.7 8.1 %copy.107 = f32[768,2304]{1,0:T(8,128)} copy(f32[768,2304]{0,1:T(8,128)} %convolution_bitcast_fusion) | data formatting | bytes 14155776
  283.1 2.5 pad_maximum_fusion.1
  285.6 1.7 convert_reduce_fusion.3
  287.3 41.5 %all-reduce.8 = (f32[2304]{0:T(1024)}, f32[768]{0:T(1024)}, f32[768]{0:T(1024)}, f32[768]{0:T(1024)}, f32[3072]{0:T(1024)}, /*index=5*/f32[768]{0:T(1024)}, f32[768]{0:T(1024)}, f32[768]{0:T(1024)}, f32[3]{0:T(128)}) all-reduce(f32[2304]{0:T(1024)S(1)} %convert_reduce_fusion.3, ...), channel_id=6, replica_groups=mesh['dp'=8,'feat'=4] {'dp','feat'}, use_global_device_ids=true, to_apply=%region_26.27.clone | all-reduce | flops 9987 | bytes 79896
  340.1 3.6 convolution_add_fusion.3
  343.7 28.5 %reduce-scatter.16.cloned.1.call-done = f32[24,768]{1,0:T(8,128)} async-done(((f32[768,768]{1,0:T(8,128)}), f32[24,768]{1,0:T(8,128)}) %reduce-scatter.16.cloned.1.call-update) | async-done | bytes 73744 | tf_op jit(solution)/shard_map/reduce_scatter | solution.py:299
  372.1 141.7 %reduce-scatter.18.cloned.1.call-done = f32[24,3072]{1,0:T(8,128)} async-done(((f32[768,3072]{1,0:T(8,128)}), f32[24,3072]{1,0:T(8,128)}) %reduce-scatter.18.cloned.1.call-update) | async-done | bytes 294928 | tf_op jit(solution)/shard_map/reduce_scatter | solution.py:303
  513.9 141.7 %reduce-scatter.20.cloned.1.call-done = f32[96,768]{1,0:T(8,128)} async-done(((f32[3072,768]{1,0:T(8,128)}), f32[96,768]{1,0:T(8,128)}) %reduce-scatter.20.cloned.1.call-update) | async-done | bytes 294928 | tf_op jit(solution)/shard_map/reduce_scatter | solution.py:305
  655.5 124.8 %reduce-scatter.22.cloned.1.call-done = f32[24,2304]{1,0:T(8,128)} async-done(((f32[768,2304]{1,0:T(8,128)}), f32[24,2304]{1,0:T(8,128)}) %reduce-scatter.22.cloned.1.call-update) | async-done | bytes 221200
  (226 shorter events, 47.7 us)
Async XLA Ops:
  7.2 5.2 copy-start.57
  7.2 45.5 %all-gather.3.cloned.1.call-start = ((), (), s32[]{:S(2)}) async-start(), calls=%async_computation.7 | async-start | bytes 5898240 | tf_op jit(solution)/shard_map/all_gather | solution.py:159
  12.4 106.9 %reduce-scatter.12.cloned.1.call-start = ((), (), s32[]{:S(2)}) async-start(), calls=%async_computation.9 | async-start | bytes 40960 | tf_op jit(solution)/shard_map/reduce_scatter | solution.py:198
  14.0 75.4 %copy-start.48 = (f32[1024]{0:T(1024)}, f32[1024]{0:T(1024)S(1)}, u32[]{:S(2)}) copy-start(f32[1024]{0:T(1024)S(1)} %fusion.78) | copy-start | bytes 12292
  67.6 6.3 copy-start.5
  67.6 6.3 copy-start.16
  67.6 6.3 copy-start.62
  69.6 7.3 copy-start.26
  88.7 4.0 copy-start.13
  89.4 3.2 copy-start.64
  92.6 2.6 copy-start.7
  92.6 3.3 copy-start.44
  92.6 4.1 copy-start.42
  92.7 2.5 copy-start.39
  92.7 2.5 copy-start.10
  92.7 2.5 copy-start.28
  98.5 51.3 %reduce-scatter.10.cloned.1.call-start = ((), (), s32[]{:S(2)}) async-start(), calls=%async_computation.8 | async-start | bytes 1966080 | tf_op jit(solution)/shard_map/reduce_scatter | solution.py:192
  98.5 2.3 copy-start.2
  98.5 2.3 copy-start.33
  105.2 91.9 %all-gather.5.cloned.1.call-start = ((), (), s32[]{:S(2)}) async-start(), calls=%async_computation.10 | async-start | bytes 1966080 | tf_op jit(solution)/shard_map/all_gather | solution.py:256
  123.8 29.4 %copy-start.35 = (f32[768]{0:T(1024)S(1)}, f32[768]{0:T(1024)}, u32[]{:S(2)}) copy-start(f32[768]{0:T(1024)} %param.22) | copy-start | bytes 9220
  123.8 29.4 %copy-start.36 = (f32[768]{0:T(1024)S(1)}, f32[768]{0:T(1024)}, u32[]{:S(2)}) copy-start(f32[768]{0:T(1024)} %param.23) | copy-start | bytes 9220
  149.8 3.4 copy-start.67
  149.8 13.4 %slice-start = ((s8[4718592]{0:T(1024)(128)(4,1)}), s8[4194304]{0:T(1024)(128)(4,1)S(1)}, s32[]{:S(2)}) async-start(s8[4718592]{0:T(1024)(128)(4,1)} %bitcast.150), calls=%async_computation.16 | async-start | bytes 8388608
  152.9 20.8 %copy-start.12 = (f32[256,768]{1,0:T(8,128)}, f32[256,768]{1,0:T(8,128)S(1)}, u32[]{:S(2)}) copy-start(f32[256,768]{1,0:T(8,128)S(1)} %get-tuple-element.116) | copy-start | bytes 2359300
  153.0 20.8 %copy-start.40 = (f32[256]{0:T(256)}, f32[256]{0:T(256)S(1)}, u32[]{:S(2)}) copy-start(f32[256]{0:T(256)S(1)} %broadcast_multiply_fusion.5) | copy-start | bytes 3076
  153.2 20.5 %copy-start.52 = (f32[256]{0:T(256)}, f32[256]{0:T(256)S(1)}, u32[]{:S(2)}) copy-start(f32[256]{0:T(256)S(1)} %fusion.81) | copy-start | bytes 3076
  153.2 10.0 %slice-start.1 = ((s8[4718592]{0:T(1024)(128)(4,1)}), s8[524288]{0:T(1024)(128)(4,1)S(1)}, s32[]{:S(2)}) async-start(s8[4718592]{0:T(1024)(128)(4,1)} %bitcast.150), calls=%async_computation.17 | async-start | bytes 1048576
  153.2 10.0 %copy-start.68 = (f32[768]{0:T(1024)S(1)}, f32[768]{0:T(1024)}, u32[]{:S(2)}) copy-start(f32[768]{0:T(1024)} %param.27) | copy-start | bytes 9220
  163.2 2.4 copy-start.22
  163.2 2.4 copy-start.46
  163.3 2.4 copy-start.50
  163.3 3.5 copy-start.56
  166.7 4.7 slice-start.2
  168.7 2.7 copy-start.21
  168.7 2.7 slice-start.3
  171.4 2.3 copy-start.23
  177.3 89.1 %reduce-scatter.14.cloned.1.call-start = ((), (), s32[]{:S(2)}) async-start(), calls=%async_computation.11 | async-start | bytes 5898240 | tf_op jit(solution)/shard_map/reduce_scatter | solution.py:288
  199.8 2.6 copy-start.3
  199.8 2.8 copy-start.15
  199.8 3.4 copy-start.25
  218.5 3.4 copy-start.41
  218.5 3.4 copy-start.53
  218.5 153.6 %reduce-scatter.16.cloned.1.call-start = ((), (), s32[]{:S(2)}) async-start(), calls=%async_computation.12 | async-start | bytes 2433024 | tf_op jit(solution)/shard_map/reduce_scatter | solution.py:299
  221.8 292.1 %reduce-scatter.18.cloned.1.call-start = ((), (), s32[]{:S(2)}) async-start(), calls=%async_computation.13 | async-start | bytes 9732096 | tf_op jit(solution)/shard_map/reduce_scatter | solution.py:303
  229.8 425.7 %reduce-scatter.20.cloned.1.call-start = ((), (), s32[]{:S(2)}) async-start(), calls=%async_computation.14 | async-start | bytes 9732096 | tf_op jit(solution)/shard_map/reduce_scatter | solution.py:305
  236.5 543.9 %reduce-scatter.22.cloned.1.call-start = ((), (), s32[]{:S(2)}) async-start(), calls=%async_computation.15 | async-start | bytes 7299072
  279.8 7.5 copy-start.47
  (34 other events, 60.0 us)
Sparse Core Ops, SparseCore 0:
  12.5 40.1 all-gather.2
  98.6 20.6 reduce-scatter.11
  121.8 27.9 reduce-scatter.9
  177.4 19.6 all-gather.4
  218.6 47.7 reduce-scatter.13
  272.1 99.9 reduce-scatter.15
  378.6 135.2 reduce-scatter.17
  520.3 135.1 reduce-scatter.19
  661.8 118.5 reduce-scatter.21
where the time goes:
time: 797 us; the launch traced here: 787 us
  waiting for transfers between devices  548 us (69%)
  matrix products  81.5 us (10%)
  blocking collectives  58.7 us (7%)
  local copies, waits for them, and re-layouts  52.5 us (7%)
  other arithmetic  30.5 us (4%)
  between operations  15.8 us (2%)
    reduce_scatter x1, waiting for transfers between devices, on_device(): lax.psum_scatter(grad_up, ('dp', 'feat'), scatter_dimension=0, tiled=True)  142 us
    reduce_scatter x1, waiting for transfers between devices, on_device(): lax.psum_scatter(grad_down, ('dp', 'feat'), scatter_dimension=0, tiled=True)  142 us
    unnamed x10, waiting for transfers between devices  125 us
    unnamed x1, blocking collectives  41.5 us
    all_gather x1, waiting for transfers between devices, on_device(): joint_rows = lax.all_gather(joint_local, 'feat', axis=0, tiled=True)  36.7 us
    reduce_scatter x1, waiting for transfers between devices, on_device(): lax.psum_scatter(joint_back.astype(jnp.bfloat16), 'feat', scatter_dimensi...  29.6 us
    reduce_scatter x1, waiting for transfers between devices, on_device(): lax.psum_scatter(grad_output, ('dp', 'feat'), scatter_dimension=0, tiled=...  28.5 us
    unnamed x155, local copies, waits for them, and re-layouts  27.2 us
  transfers between devices with their start and end apart: 9, of which 9 were waited for; matrix products, arithmetic and copies ran while one was open for 10% of the time, Pallas kernels for 0%

commit v1 on v0

v1 whole, which is shorter than its diff:
```python
import jax
import jax.numpy as jnp
from jax import lax
from jax.sharding import PartitionSpec as P

epsilon = 1e-06
f32 = jnp.float32
bf16 = jnp.bfloat16


def mm(spec, a, b):
    return jnp.einsum(spec, a, b, preferred_element_type=f32)


def layer_norm_parts(v):
    center = v - jnp.mean(v, -1, keepdims=True)
    inv = lax.rsqrt(jnp.mean(center * center, -1, keepdims=True) + epsilon)
    return center * inv, inv


def layer_norm_back(grad, normal, inv, gain):
    scaled = grad * gain
    return inv * (
        scaled
        - jnp.mean(scaled, -1, keepdims=True)
        - normal * jnp.mean(scaled * normal, -1, keepdims=True)
    )


def attention_forward(qkv, features, valid, heads, size):
    rows = qkv.shape[0]
    model = heads * size
    scale = size ** (-0.25)
    norm = features.shape[1] ** (-0.5)
    q, k, v = (
        qkv[:, i * model : (i + 1) * model].reshape(rows, heads, size).transpose(1, 0, 2)
        for i in range(3)
    )
    qw, kw = q.astype(f32), k.astype(f32)
    q_shift = scale * mm("htd,hmd->htm", q, features) - (
        scale * scale / 2 * jnp.sum(qw * qw, -1, keepdims=True)
    )
    k_shift = scale * mm("htd,hmd->htm", k, features) - (
        scale * scale / 2 * jnp.sum(kw * kw, -1, keepdims=True)
    )
    q_top = jnp.max(q_shift, -1, keepdims=True)
    k_top = lax.pmax(jnp.max(k_shift, axis=(1, 2)), "feat")[:, None, None]
    q_raw = jnp.exp(q_shift - q_top) * norm
    k_raw = jnp.exp(k_shift - k_top) * norm * valid
    q_feat, k_feat = q_raw.astype(bf16), k_raw.astype(bf16)
    state = lax.psum(mm("htm,htd->hmd", k_feat, v), "feat").astype(bf16)
    totals = lax.psum(jnp.sum(k_feat.astype(f32), 1), "feat")
    numer = mm("htm,hmd->htd", q_feat, state) * valid
    denom = jnp.sum(q_feat.astype(f32) * totals[:, None, :], -1, keepdims=True) * valid
    safe = denom + (1.0 - valid)
    attention = (numer / safe).astype(bf16).transpose(1, 0, 2).reshape(rows, model)
    return attention, (q, k, v, q_raw, k_raw, state, totals, numer, safe)


def attention_backward(g_att, saved, features, valid, heads, size):
    q, k, v, q_raw, k_raw, state, totals, numer, safe = saved
    rows = g_att.shape[0]
    scale = size ** (-0.25)
    g_att = g_att.reshape(rows, heads, size).transpose(1, 0, 2)
    q_feat, k_feat = q_raw.astype(bf16), k_raw.astype(bf16)
    g_num = (g_att / safe * valid).astype(bf16)
    g_den = (-jnp.sum(g_att * numer, -1, keepdims=True) / (safe * safe) * valid).astype(bf16)
    g_den = g_den.astype(f32)
    g_state = lax.psum(mm("htm,htd->hmd", q_feat, g_num), "feat").astype(bf16)
    g_totals = lax.psum(jnp.sum(q_feat.astype(f32) * g_den, 1), "feat")
    g_aq = (mm("htd,hmd->htm", g_num, state) + g_den * totals[:, None, :]) * q_raw
    g_ak = (mm("htd,hmd->htm", v, g_state) + g_totals[:, None, :]) * k_raw
    g_v = mm("htm,hmd->htd", k_feat, g_state)

    def back(g_a, x):
        return scale * mm("htm,hmd->htd", g_a.astype(bf16), features) - (
            scale * scale * x.astype(f32) * jnp.sum(g_a, -1, keepdims=True)
        )

    parts = [back(g_aq, q), back(g_ak, k), g_v]
    return jnp.concatenate(
        [p.astype(bf16).transpose(1, 0, 2).reshape(rows, heads * size) for p in parts], axis=1
    )


def on_device(
    tokens,
    lengths,
    joint_weight,
    joint_bias,
    output_weight,
    output_bias,
    first_gain,
    first_shift,
    up_weight,
    up_bias,
    down_weight,
    down_bias,
    second_gain,
    second_shift,
    feature_matrix,
    cotangent,
):
    model = tokens.shape[1]
    heads, _, size = feature_matrix.shape
    both = ("dp", "feat")
    row_lengths = lax.dynamic_index_in_dim(lengths, lax.axis_index("dp"), 0, keepdims=False)
    valid = (row_lengths[0] > 0).astype(f32)
    features = lax.all_gather(feature_matrix, "feat", axis=1, tiled=True)
    qkv = (mm("td,de->te", tokens, joint_weight) + joint_bias).astype(bf16)
    attention, saved = attention_forward(qkv, features, valid, heads, size)
    branch_attn = mm("td,de->te", attention, output_weight) + output_bias
    wide = tokens.astype(f32)
    normal_1, inv_1 = layer_norm_parts(wide + branch_attn)
    hidden = normal_1 * first_gain + first_shift
    hidden_low = hidden.astype(bf16)
    pre = mm("td,df->tf", hidden_low, up_weight) + up_bias
    half_erf = 0.5 * (1.0 + lax.erf(pre * (0.5**0.5)))
    slope = half_erf + pre * jnp.exp(-0.5 * pre * pre) * 0.3989422804014327
    activated = (pre * half_erf).astype(bf16)
    branch_ffn = mm("tf,fd->td", activated, down_weight) + down_bias
    normal_2, inv_2 = layer_norm_parts(hidden + branch_ffn)
    layer_output = ((normal_2 * second_gain + second_shift) * valid).astype(bf16)
    moments = valid * jnp.stack(
        [jnp.sum(wide * wide), jnp.sum(branch_attn * branch_attn), jnp.sum(branch_ffn * branch_ffn)]
    )
    g_out = cotangent.astype(f32) * valid
    grad_secondgain = jnp.sum(g_out * normal_2, 0)
    grad_secondshift = jnp.sum(g_out, 0)
    g_second = layer_norm_back(g_out, normal_2, inv_2, second_gain)
    g_ffn = g_second.astype(bf16)
    grad_down = mm("tf,td->fd", activated, g_ffn)
    grad_downbias = jnp.sum(g_ffn.astype(f32), 0)
    g_pre = (mm("td,fd->tf", g_ffn, down_weight) * slope).astype(bf16)
    grad_up = mm("td,tf->df", hidden_low, g_pre)
    grad_upbias = jnp.sum(g_pre.astype(f32), 0)
    g_hidden = g_second + mm("tf,df->td", g_pre, up_weight)
    grad_firstgain = jnp.sum(g_hidden * normal_1, 0)
    grad_firstshift = jnp.sum(g_hidden, 0)
    g_first = layer_norm_back(g_hidden, normal_1, inv_1, first_gain)
    g_branch = g_first.astype(bf16)
    grad_output = mm("td,te->de", attention, g_branch)
    grad_outputbias = jnp.sum(g_branch.astype(f32), 0)
    g_att = mm("te,de->td", g_branch, output_weight)
    g_qkv = attention_backward(g_att, saved, features, valid, heads, size)
    grad_joint = mm("td,te->de", tokens, g_qkv)
    grad_jointbias = jnp.sum(g_qkv.astype(f32), 0)
    input_gradient = g_first + mm("te,de->td", g_qkv, joint_weight)

    shards = lax.axis_size(both)
    small = jnp.concatenate(
        [
            p.reshape(shards, -1)
            for p in (
                grad_jointbias,
                grad_outputbias,
                grad_firstgain,
                grad_firstshift,
                grad_upbias,
                grad_downbias,
                grad_secondgain,
                grad_secondshift,
            )
        ]
        + [jnp.broadcast_to(moments, (shards, 3))],
        axis=1,
    )
    small = lax.psum_scatter(small, both, scatter_dimension=0, tiled=True)[0]
    each = model // shards
    cuts, at = [], 0
    for width in (3 * each, each, each, each, up_bias.shape[0] // shards, each, each, each, 3):
        cuts.append(small[at : at + width])
        at += width

    def scatter(partial):
        return lax.psum_scatter(
            partial.astype(bf16), both, scatter_dimension=0, tiled=True
        ).astype(f32)

    valid_count = jnp.sum(lengths).astype(f32)
    token_moments = jnp.sqrt(cuts[8] / (valid_count * model))
    return (
        layer_output,
        input_gradient,
        scatter(grad_joint),
        cuts[0],
        scatter(grad_output),
        cuts[1],
        cuts[2],
        cuts[3],
        scatter(grad_up),
        cuts[4],
        scatter(grad_down),
        cuts[5],
        cuts[6],
        cuts[7],
        token_moments,
    )


def solution(mesh):
    rows = P(("dp", "feat"), None)
    flat = P(("dp", "feat"))
    in_specs = (rows,) + (P(),) * 13 + (P(None, "feat", None), rows)
    out_specs = (rows, rows, rows, flat, rows, flat, flat, flat, rows, flat, rows, flat, flat, flat, P())
    return jax.shard_map(
        on_device, mesh=mesh, in_specs=in_specs, out_specs=out_specs, check_vma=False
    )
```

time: 797 us -> 538 us (0.68)
  waiting for transfers between devices: 548 us -> 297 us
  blocking collectives: 58.7 us -> 99.6 us
  matrix products: 81.5 us -> 59.2 us
  local copies, waits for them, and re-layouts: 52.5 us -> 40.4 us
    reduce_scatter x6 -> x3, waiting for transfers between devices: 381 us -> 218 us  [scatter(): lax.psum_scatter(partial.astype(bf16), both, scatter_dimension=0, tiled=T...]
    unnamed x10 -> x5, waiting for transfers between devices: 125 us -> 78.9 us
    all_gather x2 -> x0, waiting for transfers between devices: 41.8 us -> none  [the longest x1 36.7 us: on_device(): joint_rows = lax.all_gather(joint_local, 'feat', axis=0, tiled=True)]
    psum x0 -> x2, blocking collectives: none -> 40.9 us  [the longest x1 20.8 us: attention_backward(): g_state = lax.psum(mm('htm,htd->hmd', q_feat, g_num), 'feat').astype(bf16)]
    dot_general x32 -> x21, matrix products: 81.5 us -> 53.6 us  [mm(): return jnp.einsum(spec, a, b, preferred_element_type=f32)]
    unnamed x155 -> x97, local copies, waits for them, and re-layouts: 27.2 us -> 15.7 us
    reshape x0 -> x8, local copies, waits for them, and re-layouts: none -> 10.4 us  [on_device(): p.reshape(shards, -1)]
    reduce_sum x15 -> x12, other arithmetic: 16.3 us -> 13.8 us  [the longest x1 3.45 us: attention_forward(): totals = lax.psum(jnp.sum(k_feat.astype(f32), 1), 'feat')]
  transfers between devices with their start and end apart: 9 -> 4, of which waited for: 9 -> 3; matrix products, arithmetic and copies ran while one was open for 10% -> 12% of each run, Pallas kernels for 0% -> 0%
where the time goes in v1:
time: 538 us; the launch traced here: 536 us
  waiting for transfers between devices  297 us (55%)
  blocking collectives  99.6 us (19%)
  matrix products  59.2 us (11%)
  local copies, waits for them, and re-layouts  40.4 us (8%)
  other arithmetic  24.1 us (4%)
  between operations  15.6 us (3%)
    reduce_scatter x3, waiting for transfers between devices, scatter(): lax.psum_scatter(partial.astype(bf16), both, scatter_dimension=0, tiled=T...  218 us
    unnamed x5, waiting for transfers between devices  78.9 us
    dot_general x21, matrix products, mm(): return jnp.einsum(spec, a, b, preferred_element_type=f32)  53.6 us
    unnamed x1, blocking collectives  41 us
    psum x1, blocking collectives, attention_backward(): g_state = lax.psum(mm('htm,htd->hmd', q_feat, g_num), 'feat').astype(bf16)  20.8 us
    psum x1, blocking collectives, attention_forward(): state = lax.psum(mm('htm,htd->hmd', k_feat, v), 'feat').astype(bf16)  20.2 us
    unnamed x97, local copies, waits for them, and re-layouts  15.7 us
  transfers between devices with their start and end apart: 4, of which 3 were waited for; matrix products, arithmetic and copies ran while one was open for 12% of the time, Pallas kernels for 0%

profile of v1, /device:TPU:0, one launch (start us, length us, event | category | flops | bytes accessed | tf_op | source)
XLA Modules:
  0.0 536.2 jit_solution(14769303694368289689)
XLA Ops:
  9.3 2.1 fusion.3
  12.4 1.9 copy.62
  15.5 10.3 %all_gather.3 = bf16[12,256,64]{2,1,0:T(8,128)(2,1)S(1)} all-gather(bf16[12,64,64]{2,1,0:T(8,128)(2,1)} %param.30), channel_id=1, replica_groups=mesh['dp'=8,'feat'=4] {'feat'}, dimensions={1}, use_global_device_ids=true | all-gather | bytes 491520 | tf_op jit(solution)/shard_map/all_gather | solution.py:109
  26.7 3.7 fusion.10
  30.4 7.3 %pmax.7 = f32[12]{0:T(128)} all-reduce(f32[12]{0:T(128)} %get-tuple-element.97), channel_id=1, replica_groups=mesh['dp'=8,'feat'=4] {'feat'}, use_global_device_ids=true, to_apply=%region_4.5 | all-reduce | flops 12 | bytes 96 | tf_op jit(solution)/shard_map/pmax | solution.py:47
  37.7 1.9 copy.64
  39.7 3.4 convert_reduce_fusion.1
  44.3 1.5 fusion.73
  45.8 1.9 copy.61
  49.4 20.2 %all-reduce.5 = (bf16[12,256,64]{1,2,0:T(8,128)(2,1)}, f32[12,256]{1,0:T(8,128)}) all-reduce(f32[12,256,64]{1,2,0:T(8,128)} %fusion.73, f32[12,256]{1,0:T(8,128)} %get-tuple-element.82), channel_id=1, replica_groups=mesh['dp'=8,'feat'=4] {'feat'}, use_global_device_ids=true, to_apply=%region_5.6 | all-reduce | flops 199680 | bytes 1204224 | tf_op jit(solution)/shard_map/psum | solution.py:51
  69.6 5.5 %fusion.4 = (f32[12,256]{1,0:T(8,128)}, bf16[12,256,256]{1,2,0:T(8,128)(2,1)}, f32[12,256,256]{1,2,0:T(8,128)}) fusion(f32[12,256]{1,0:T(8,128)} %get-tuple-element.71, f32[12,256]{1,0:T(8,128)} %broadcast_multiply_fusion.1, bf16[12,256,64]{2,1,0:T(8,128)(2,1)} %copy-done.3, bf16[12,256,64]{1,2,0:T(8,128)(2,1)} %bitcast.106), kind=kOutput, calls=%fused_computation.13 | convolution fusion | flops 106955008 | bytes 5541888 | tf_op jit(solution)/shard_map/sub | solution.py:48
  76.0 2.8 fusion.44
  80.4 4.0 multiply_convert_fusion
  84.5 2.2 fusion.66
  87.9 1.7 convert_reduce_fusion.3
  89.6 3.0 convert_reduce_fusion
  92.6 2.3 multiply_reduce_fusion.3
  96.7 1.5 convolution_convert_fusion.3
  98.3 2.1 fusion.58
  101.2 3.1 fusion.63
  105.6 2.5 fusion.72
  108.2 20.8 %all-reduce.6 = (bf16[12,256,64]{1,2,0:T(8,128)(2,1)}, f32[12,256]{1,0:T(8,128)}) all-reduce(f32[12,256,64]{1,2,0:T(8,128)} %fusion.63, f32[12,256]{1,0:T(8,128)} %fusion.5), channel_id=1, replica_groups=mesh['dp'=8,'feat'=4] {'feat'}, use_global_device_ids=true, to_apply=%region_19.20 | all-reduce | flops 199680 | bytes 1204224 | tf_op jit(solution)/shard_map/psum | solution.py:69
  129.0 3.6 fusion.71
  135.4 2.8 fusion.1
  138.2 5.8 %copy.85 = bf16[768,2304]{1,0:T(8,128)(2,1)} copy(bf16[768,2304]{0,1:T(8,128)(2,1)} %fusion.1) | data formatting | bytes 7077888
  144.7 5.4 %convolution_convert_fusion.1 = bf16[768,3072]{1,0:T(8,128)(2,1)} fusion(bf16[256,3072]{1,0:T(8,128)(2,1)} %copy-done.18, f32[256,768]{1,0:T(8,128)} %copy-done.5, f32[768]{0:T(1024)S(1)} %copy-done.26, f32[768]{0:T(1024)S(1)} %copy-done.24, f32[256]{0:T(256)S(1)} %copy-done.32, f32[256]{0:T(256)S(1)} %copy-done.28), kind=kOutput, calls=%fused_computation.2 | convolution fusion | flops 1211301888 | bytes 7086080 | tf_op jit(solution)/shard_map/td,tf->df/dot_general | solution.py:12
  150.2 5.2 convolution_convert_fusion
  156.7 2.2 convert_reduce_fusion.2
  159.8 1.4 reshape.192
  161.1 1.4 reshape.193
  162.5 1.4 reshape.194
  163.9 1.4 reshape.195
  165.2 1.4 reshape.196
  166.6 1.4 reshape.197
  168.0 1.4 reshape.198
  170.0 2.0 maximum_multiply_fusion
  172.6 1.6 concatenate.7
  174.2 41.0 %all-reduce = f32[32,315]{1,0:T(8,128)} all-reduce(f32[32,315]{1,0:T(8,128)} %concatenate.7), channel_id=3, replica_groups=mesh['dp'=8,'feat'=4] {'dp','feat'}, use_global_device_ids=true, to_apply=%region_35.36.clone | all-reduce | flops 10080 | bytes 80640
  218.9 1.5 dynamic-slice_bitcast_fusion
  220.4 3.6 convolution_add_fusion.3
  223.9 1.4 convert_element_type.193
  225.4 78.8 %reduce-scatter.13.cloned.1.call-done = bf16[24,2304]{1,0:T(8,128)(2,1)} async-done(((bf16[768,2304]{1,0:T(8,128)(2,1)}), bf16[24,2304]{1,0:T(8,128)(2,1)}) %reduce-scatter.13.cloned.1.call-update) | async-done | bytes 110608
  304.2 1.9 copy.86
  306.1 2.0 copy.74
  308.1 108.1 %reduce-scatter.9.cloned.1.call-done = bf16[24,3072]{1,0:T(8,128)(2,1)} async-done(((bf16[768,3072]{1,0:T(8,128)(2,1)}), bf16[24,3072]{1,0:T(8,128)(2,1)}) %reduce-scatter.9.cloned.1.call-update) | async-done | bytes 147472 | tf_op jit(solution)/shard_map/reduce_scatter | solution.py:176
  416.2 1.6 convert_element_type.195
  417.8 110.2 %reduce-scatter.11.cloned.1.call-done = bf16[96,768]{1,0:T(8,128)(2,1)} async-done(((bf16[3072,768]{1,0:T(8,128)(2,1)}), bf16[96,768]{1,0:T(8,128)(2,1)}) %reduce-scatter.11.cloned.1.call-update) | async-done | bytes 147472 | tf_op jit(solution)/shard_map/reduce_scatter | solution.py:176
  528.1 1.6 convert_element_type.197
  (140 shorter events, 24.9 us)
Async XLA Ops:
  7.2 2.1 copy-start
  7.2 216.8 %reduce-scatter.7.cloned.1.call-start = ((), (), s32[]{:S(2)}) async-start(), calls=%async_computation.4 | async-start | bytes 1216512 | tf_op jit(solution)/shard_map/reduce_scatter | solution.py:176
  25.8 0.9 copy-start.3
  39.7 4.7 copy-start.16
  43.1 1.2 copy-start.1
  75.2 3.7 copy-start.19
  75.2 3.7 copy-start.35
  75.2 3.7 copy-start.40
  78.8 1.5 copy-start.23
  78.8 1.5 copy-start.25
  78.8 1.5 copy-start.39
  80.1 14.8 %copy-start.5 = (f32[256,768]{1,0:T(8,128)}, f32[256,768]{1,0:T(8,128)S(1)}, u32[]{:S(2)}) copy-start(f32[256,768]{1,0:T(8,128)S(1)} %get-tuple-element.79) | copy-start | bytes 2359300
  80.1 14.8 %copy-start.27 = (f32[256]{0:T(256)}, f32[256]{0:T(256)S(1)}, u32[]{:S(2)}) copy-start(f32[256]{0:T(256)S(1)} %broadcast_multiply_fusion.7) | copy-start | bytes 3076
  80.1 4.4 slice-start
  80.3 14.6 %copy-start.31 = (f32[256]{0:T(256)}, f32[256]{0:T(256)S(1)}, u32[]{:S(2)}) copy-start(f32[256]{0:T(256)S(1)} %add_rsqrt_fusion.1) | copy-start | bytes 3076
  80.3 4.1 slice-start.1
  80.3 4.1 copy-start.41
  84.4 2.2 copy-start.8
  84.5 2.4 copy-start.17
  84.5 2.4 copy-start.29
  84.5 3.4 copy-start.33
  87.9 4.7 slice-start.2
  89.6 3.0 copy-start.10
  89.6 3.0 slice-start.3
  92.6 2.3 copy-start.18
  95.8 0.9 copy-start.6
  98.2 206.0 %reduce-scatter.13.cloned.1.call-start = ((), (), s32[]{:S(2)}) async-start(), calls=%async_computation.7 | async-start | bytes 3649536
  98.3 6.0 %copy-start.20 = (f32[12,256,64]{1,2,0:T(8,128)S(1)}, f32[12,256,64]{1,2,0:T(8,128)}, u32[]{:S(2)}) copy-start(f32[12,256,64]{1,2,0:T(8,128)} %get-tuple-element.101) | copy-start | bytes 2359300
  100.4 4.1 copy-start.22
  100.4 4.1 copy-start.11
  101.2 4.4 copy-start.37
  101.2 4.4 copy-start.38
  101.2 4.4 copy-start.42
  128.9 3.6 copy-start.30
  128.9 3.7 copy-start.2
  128.9 3.7 copy-start.21
  129.0 4.1 copy-start.4
  129.0 4.1 copy-start.7
  132.6 1.0 copy-start.9
  132.6 1.7 copy-start.12
  133.0 1.6 copy-start.13
  133.1 2.3 copy-start.36
  133.5 1.2 copy-start.14
  134.6 0.8 copy-start.15
  144.0 0.7 copy-start.28
  144.0 0.7 copy-start.32
  144.1 272.1 %reduce-scatter.9.cloned.1.call-start = ((), (), s32[]{:S(2)}) async-start(), calls=%async_computation.5 | async-start | bytes 4866048 | tf_op jit(solution)/shard_map/reduce_scatter | solution.py:176
  150.1 377.9 %reduce-scatter.11.cloned.1.call-start = ((), (), s32[]{:S(2)}) async-start(), calls=%async_computation.6 | async-start | bytes 4866048 | tf_op jit(solution)/shard_map/reduce_scatter | solution.py:176
  (3 other events, 2.1 us)
Sparse Core Ops, SparseCore 0:
  98.3 97.7 reduce-scatter.6
  201.6 102.5 reduce-scatter.12
  309.7 106.4 reduce-scatter.8
  421.5 106.5 reduce-scatter.10

commit v2 on v1

--- a/solution.py
+++ b/solution.py
@@ -1,6 +1,10 @@
+import functools
+
 import jax
 import jax.numpy as jnp
 from jax import lax
+from jax.experimental import pallas as pl
+from jax.experimental.pallas import tpu as pltpu
 from jax.sharding import PartitionSpec as P
 
 epsilon = 1e-06
@@ -81,6 +85,290 @@
     return jnp.concatenate(
         [p.astype(bf16).transpose(1, 0, 2).reshape(rows, heads * size) for p in parts], axis=1
     )
+
+
+MESH = pl.DeviceIdType.MESH
+
+
+class Chunk:
+    def __init__(self, part, first, r, w, kind, bufs, sems):
+        self.part, self.first, self.r, self.w, self.kind = part, first, r, w, kind
+        self.b1, self.b2, self.b3, self.fin, self.got = bufs
+        self.sems = sems
+
+
+def plan(tokens, joint, up):
+    half_joint, half_up, half = joint // 2, up // 2, tokens // 2
+    return (
+        ("up", half_up // 3, 3),
+        ("down", half // 3, 3),
+        ("output", half, 1),
+        ("joint", half_joint // 3, 3),
+    )
+
+
+def scatter_kernel(chips, model, *refs):
+    (tok, att, hid, act, g_qkv, g_branch, g_pre, g_ffn, small) = refs[:9]
+    outs = dict(zip(("joint", "output", "up", "down", "small"), refs[9:14]))
+    scratch = list(refs[14:])
+    pair = dict(zip(("tok", "att", "hid", "act", "qkv", "branch", "pre", "ffn", "small"), scratch[:9]))
+    parts = dict(zip(("up", "down", "output", "joint", "small"), scratch[9:14]))
+    pair_send, pair_recv, send, recv = scratch[14:18]
+    rest = scratch[18:]
+
+    dp, feat = lax.axis_index("dp"), lax.axis_index("feat")
+    depth = chips // 4
+    z, x, y, c = dp // 2, dp % 2, feat // 2, feat % 2
+    core = (dp, y * 2 + 1 - c)
+
+    def route(turn):
+        return (
+            (x + turn * (y - x), 2 - turn),
+            (y + turn * (x - y), 1 + turn),
+            (z * 2 + x + (1 - turn) * (1 - 2 * x), (y + turn * (1 - 2 * y)) * 2 + c),
+            (z * 2 + x + turn * (1 - 2 * x), (y + (1 - turn) * (1 - 2 * y)) * 2 + c),
+        )
+
+    routes = {False: route(c), True: route(0)}
+
+    def along(k):
+        return ((z + k) % depth * 2 + x, feat)
+
+    barrier = pltpu.get_barrier_semaphore()
+    greeted = [core, *routes[False][2:]] + [along(k) for k in range(1, depth)]
+    for device in greeted:
+        pl.semaphore_signal(barrier, inc=1, device_id=device, device_id_type=MESH)
+    pl.semaphore_wait(barrier, len(greeted))
+
+    def halves(ref):
+        width = ref.shape[1] // 2
+        return ref.at[:, pl.ds(pl.multiple_of((1 - c) * width, 128), width)]
+
+    exchange = []
+    sources = (
+        ("small", small.at[:, 1 - c]),
+        ("hid", hid),
+        ("pre", halves(g_pre)),
+        ("ffn", halves(g_ffn)),
+        ("act", act),
+        ("att", att),
+        ("branch", halves(g_branch)),
+        ("tok", tok),
+        ("qkv", halves(g_qkv)),
+    )
+    arrived = {}
+    for i, (name, source) in enumerate(sources):
+        copy = pltpu.make_async_remote_copy(
+            src_ref=source,
+            dst_ref=pair[name],
+            send_sem=pair_send.at[i],
+            recv_sem=pair_recv.at[i],
+            device_id=core,
+            device_id_type=MESH,
+        )
+        copy.start()
+        arrived[name] = copy
+
+    factors = {
+        "up": (hid, "hid", g_pre, "pre"),
+        "down": (act, "act", g_ffn, "ffn"),
+        "output": (att, "att", g_branch, "branch"),
+        "joint": (tok, "tok", g_qkv, "qkv"),
+    }
+
+    chunks = []
+    todo = [("small", 128, 1)] + list(plan(model, g_qkv.shape[1], g_pre.shape[1]))
+    at = 0
+    for name, w, count in todo:
+        for k in range(count):
+            part = parts[name]
+            r = part.shape[0] // chips
+            chunks.append(Chunk(part, k * w, r, w, name, rest[5 * at : 5 * at + 5], at))
+            at += 1
+
+    def product(name, columns, w):
+        left, left_pair, right, right_pair = factors[name]
+        for item in (left_pair, right_pair):
+            if item in arrived:
+                arrived.pop(item).wait_recv()
+        own = right[:, pl.ds(pl.multiple_of(c * (right.shape[1] // 2) + columns, 128), w)]
+        other = pair[right_pair][:, columns : columns + w]
+        dims = (((0,), (0,)), ((), ()))
+        tile = 256
+
+        @pl.loop(0, left.shape[1] // tile)
+        def _(i):
+            rows = pl.ds(pl.multiple_of(i * tile, tile), tile)
+            total = lax.dot_general(left[:, rows], own, dims, preferred_element_type=f32)
+            total += lax.dot_general(
+                pair[left_pair][:, rows], other, dims, preferred_element_type=f32
+            )
+            parts[name][rows, columns : columns + w] = total.astype(bf16)
+
+    def block(chunk, zb, pb, sb):
+        (_, step_p), (_, step_s), _, _ = routes[chunk.kind == "small"]
+        q = 4 * zb + step_p * pb + step_s * sb
+        rows = pl.ds(pl.multiple_of(q * chunk.r, min(chunk.r, 16)), chunk.r)
+        return chunk.part.at[rows, pl.ds(chunk.first, chunk.w)]
+
+    def start(source, target, chunk, stage, device):
+        pltpu.make_async_remote_copy(
+            src_ref=source,
+            dst_ref=target,
+            send_sem=send.at[chunk.sems, stage],
+            recv_sem=recv.at[chunk.sems, stage],
+            device_id=device,
+            device_id_type=MESH,
+        ).start()
+
+    def done(sems, chunk, stage, ref):
+        pltpu.make_async_copy(ref, ref, sems.at[chunk.sems, stage]).wait()
+
+    def places(chunk):
+        (p, _), (s, _), first, second = routes[chunk.kind == "small"]
+        return p, s, first, second
+
+    made = set()
+
+    def stage_0(chunk):
+        if chunk.kind == "small":
+            arrived.pop("small").wait_recv()
+            chunk.part[...] = (small[:, c] + pair["small"][...]).reshape(chunk.part.shape)
+        elif chunk.kind == "down":
+            if "down" not in made:
+                made.add("down")
+                product("down", 0, chunk.part.shape[1])
+        else:
+            product(chunk.kind, chunk.first, chunk.w)
+        p, _, first, _ = places(chunk)
+        for zb in range(depth):
+            for sb in range(2):
+                start(block(chunk, zb, 1 - p, sb), chunk.b1.at[2 * zb + sb], chunk, 0, first)
+
+    def stage_1(chunk):
+        p, s, _, second = places(chunk)
+        done(recv, chunk, 0, chunk.b1)
+        for zb in range(depth):
+            for sb in range(2):
+                i = 2 * zb + sb
+                total = chunk.b1[i].astype(f32) + block(chunk, zb, p, sb)[...].astype(f32)
+                chunk.b1[i] = total.astype(chunk.b1.dtype)
+        for zb in range(depth):
+            start(chunk.b1.at[2 * zb + 1 - s], chunk.b2.at[zb], chunk, 1, second)
+
+    def stage_2(chunk):
+        _, s, _, _ = places(chunk)
+        done(recv, chunk, 1, chunk.b2)
+        for zb in range(depth):
+            total = chunk.b2[zb].astype(f32) + chunk.b1[2 * zb + s].astype(f32)
+            chunk.b2[zb] = total.astype(chunk.b2.dtype)
+        for k in range(1, depth):
+            start(chunk.b2.at[(z + k) % depth], chunk.b3.at[z], chunk, 2, along(k))
+        chunk.b3[z] = chunk.b2[z]
+
+    def stage_3(chunk):
+        done(recv, chunk, 2, chunk.b3.at[pl.ds(0, depth - 1)])
+        total = chunk.b3[0].astype(f32)
+        for k in range(1, depth):
+            total += chunk.b3[k].astype(f32)
+        if chunk.kind == "small":
+            outs["small"][...] = total
+            return
+        chunk.fin[...] = total
+        half = chunk.r // 2
+        start(chunk.fin.at[pl.ds(pl.multiple_of((1 - c) * half, 8), half)], chunk.got, chunk, 3, core)
+
+    def stage_4(chunk):
+        if chunk.kind == "small":
+            return
+        done(recv, chunk, 3, chunk.got)
+        out = outs[chunk.kind]
+        width = out.shape[1] // 2
+        half = chunk.r // 2
+
+        def columns(side):
+            return pl.ds(pl.multiple_of(side * width + chunk.first, 128), chunk.w)
+
+        out[:, columns(c)] = chunk.fin[pl.ds(pl.multiple_of(c * half, 8), half), :]
+        out[:, columns(1 - c)] = chunk.got[...]
+
+    stages = ((stage_0, 0), (stage_1, 2), (stage_2, 3), (stage_3, 4), (stage_4, 5))
+    for step in range(len(chunks) + 5):
+        for stage, lag in stages:
+            if 0 <= step - lag < len(chunks):
+                stage(chunks[step - lag])
+
+    for i, (name, source) in enumerate(sources):
+        pltpu.make_async_copy(pair[name], pair[name], pair_send.at[i]).wait()
+    for chunk in chunks:
+        done(send, chunk, 0, chunk.b1)
+        done(send, chunk, 1, chunk.b2)
+        done(send, chunk, 2, chunk.b3.at[pl.ds(0, depth - 1)])
+        if chunk.kind != "small":
+            done(send, chunk, 3, chunk.got)
+
+
+def scatter_gradients(chips, tok, att, hid, act, g_qkv, g_branch, g_pre, g_ffn, small):
+    rows, model = tok.shape
+    devices = 2 * chips
+    joint, up = g_qkv.shape[1], g_pre.shape[1]
+    halved = {"qkv": joint // 2, "branch": model // 2, "pre": up // 2, "ffn": model // 2}
+    scratch = [
+        pltpu.VMEM((rows, model), bf16),
+        pltpu.VMEM((rows, model), bf16),
+        pltpu.VMEM((rows, model), bf16),
+        pltpu.VMEM((rows, up), bf16),
+        pltpu.VMEM((rows, halved["qkv"]), bf16),
+        pltpu.VMEM((rows, halved["branch"]), bf16),
+        pltpu.VMEM((rows, halved["pre"]), bf16),
+        pltpu.VMEM((rows, halved["ffn"]), bf16),
+        pltpu.VMEM((chips, 8, 128), f32),
+    ]
+    sizes = {
+        "up": (model, up // 2, bf16),
+        "down": (up, model // 2, bf16),
+        "output": (model, model // 2, bf16),
+        "joint": (model, joint // 2, bf16),
+        "small": (chips * 8, 128, f32),
+    }
+    scratch += [pltpu.VMEM(sizes[k][:2], sizes[k][2]) for k in ("up", "down", "output", "joint", "small")]
+    todo = [("small", 128, 1)] + list(plan(model, joint, up))
+    count = sum(n for _, _, n in todo)
+    scratch += [
+        pltpu.SemaphoreType.DMA((9,)),
+        pltpu.SemaphoreType.DMA((9,)),
+        pltpu.SemaphoreType.DMA((count, 4)),
+        pltpu.SemaphoreType.DMA((count, 4)),
+    ]
+    depth = chips // 4
+    for name, w, n in todo:
+        r, kind = sizes[name][0] // chips, sizes[name][2]
+        for _ in range(n):
+            scratch += [
+                pltpu.VMEM((2 * depth, r, w), kind),
+                pltpu.VMEM((depth, r, w), kind),
+                pltpu.VMEM((depth, r, w), kind),
+                pltpu.VMEM((r, w), f32),
+                pltpu.VMEM((max(r // 2, 8), w), f32),
+            ]
+    vmem = pl.BlockSpec(memory_space=pltpu.VMEM)
+    return pl.pallas_call(
+        functools.partial(scatter_kernel, chips, model),
+        out_shape=(
+            jax.ShapeDtypeStruct((model // devices, joint), f32),
+            jax.ShapeDtypeStruct((model // devices, model), f32),
+            jax.ShapeDtypeStruct((model // devices, up), f32),
+            jax.ShapeDtypeStruct((up // devices, model), f32),
+            jax.ShapeDtypeStruct((8, 128), f32),
+        ),
+        in_specs=[vmem] * 9,
+        out_specs=(vmem,) * 5,
+        scratch_shapes=scratch,
+        compiler_params=pltpu.CompilerParams(
+            collective_id=0, has_side_effects=True, vmem_limit_bytes=60 << 20
+        ),
+        name="scatter_gradients",
+    )(tok, att, hid, act, g_qkv, g_branch, g_pre, g_ffn, small)
 
 
 def on_device(
@@ -129,25 +417,23 @@
     grad_secondshift = jnp.sum(g_out, 0)
     g_second = layer_norm_back(g_out, normal_2, inv_2, second_gain)
     g_ffn = g_second.astype(bf16)
-    grad_down = mm("tf,td->fd", activated, g_ffn)
     grad_downbias = jnp.sum(g_ffn.astype(f32), 0)
     g_pre = (mm("td,fd->tf", g_ffn, down_weight) * slope).astype(bf16)
-    grad_up = mm("td,tf->df", hidden_low, g_pre)
     grad_upbias = jnp.sum(g_pre.astype(f32), 0)
     g_hidden = g_second + mm("tf,df->td", g_pre, up_weight)
     grad_firstgain = jnp.sum(g_hidden * normal_1, 0)
     grad_firstshift = jnp.sum(g_hidden, 0)
     g_first = layer_norm_back(g_hidden, normal_1, inv_1, first_gain)
     g_branch = g_first.astype(bf16)
-    grad_output = mm("td,te->de", attention, g_branch)
     grad_outputbias = jnp.sum(g_branch.astype(f32), 0)
     g_att = mm("te,de->td", g_branch, output_weight)
     g_qkv = attention_backward(g_att, saved, features, valid, heads, size)
-    grad_joint = mm("td,te->de", tokens, g_qkv)
     grad_jointbias = jnp.sum(g_qkv.astype(f32), 0)
     input_gradient = g_first + mm("te,de->td", g_qkv, joint_weight)
 
     shards = lax.axis_size(both)
+    each = model // shards
+    widths = (3 * each, each, each, each, up_bias.shape[0] // shards, each, each, each, 3)
     small = jnp.concatenate(
         [
             p.reshape(shards, -1)
@@ -165,32 +451,46 @@
         + [jnp.broadcast_to(moments, (shards, 3))],
         axis=1,
     )
-    small = lax.psum_scatter(small, both, scatter_dimension=0, tiled=True)[0]
-    each = model // shards
+    if lax.axis_size("feat") == 4 and lax.axis_size("dp") == 8 and sum(widths) <= 1024:
+        chips = shards // 2
+        packed = jnp.pad(small, ((0, 0), (0, 1024 - sum(widths)))).reshape(chips, 2, 8, 128)
+        *big, small = scatter_gradients(
+            chips, tokens, attention, hidden_low, activated, g_qkv, g_branch, g_pre, g_ffn, packed
+        )
+        small = small.reshape(-1)
+    else:
+        small = lax.psum_scatter(small, both, scatter_dimension=0, tiled=True)[0]
+        pairs = (
+            ("td,te->de", tokens, g_qkv),
+            ("td,te->de", attention, g_branch),
+            ("td,tf->df", hidden_low, g_pre),
+            ("tf,td->fd", activated, g_ffn),
+        )
+        big = [
+            lax.psum_scatter(
+                mm(spec, left, right).astype(bf16), both, scatter_dimension=0, tiled=True
+            ).astype(f32)
+            for spec, left, right in pairs
+        ]
     cuts, at = [], 0
-    for width in (3 * each, each, each, each, up_bias.shape[0] // shards, each, each, each, 3):
+    for width in widths:
         cuts.append(small[at : at + width])
         at += width
-
-    def scatter(partial):
-        return lax.psum_scatter(
-            partial.astype(bf16), both, scatter_dimension=0, tiled=True
-        ).astype(f32)
 
     valid_count = jnp.sum(lengths).astype(f32)
     token_moments = jnp.sqrt(cuts[8] / (valid_count * model))
     return (
         layer_output,
         input_gradient,
-        scatter(grad_joint),
+        big[0],
         cuts[0],
-        scatter(grad_output),
+        big[1],
         cuts[1],
         cuts[2],
         cuts[3],
-        scatter(grad_up),
+        big[2],
         cuts[4],
-        scatter(grad_down),
+        big[3],
         cuts[5],
         cuts[6],
         cuts[7],

time: 538 us -> 251 us (0.47)
  waiting for transfers between devices: 297 us -> 0 us
  Pallas kernels: 0 us -> 78.7 us
  blocking collectives: 99.6 us -> 58.6 us
  matrix products: 59.2 us -> 45.4 us
  between operations: 15.6 us -> 2.46 us
    reduce_scatter x3 -> x0, waiting for transfers between devices: 218 us -> none  [scatter(): lax.psum_scatter(partial.astype(bf16), both, scatter_dimension=0, tiled=T...]
    unnamed x5 -> x0, waiting for transfers between devices: 78.9 us -> none
    pallas_call x0 -> x1, Pallas kernels: none -> 78.7 us  [scatter_gradients(): pl.pallas_call(functools.partial(scatter_kernel, chips, model), out_shape...]
    unnamed x1 -> x0, blocking collectives: 41 us -> none
    dot_general x21 -> x17, matrix products: 53.6 us -> 40 us  [mm(): return jnp.einsum(spec, a, b, preferred_element_type=f32)]
    reshape x0 -> x4, local copies, waits for them, and re-layouts: none -> 7.68 us  [the longest x3 5.77 us: attention_backward(): p.astype(bf16).transpose(1, 0, 2).reshape(rows, heads * size)]
    unnamed x97 -> x74, local copies, waits for them, and re-layouts: 15.7 us -> 11.5 us
  transfers between devices with their start and end apart: 4 -> 0, of which waited for: 3 -> 0; matrix products, arithmetic and copies ran while one was open for 12% -> 0% of each run, Pallas kernels for 0% -> 0%
where the time goes in v2:
time: 251 us; the launch traced here: 249 us
  Pallas kernels  78.7 us (31%)
  blocking collectives  58.6 us (23%)
  matrix products  45.4 us (18%)
  local copies, waits for them, and re-layouts  43.8 us (17%)
  other arithmetic  20.5 us (8%)
    pallas_call x1, Pallas kernels, scatter_gradients(): pl.pallas_call(functools.partial(scatter_kernel, chips, model), out_shape...  78.7 us
    dot_general x17, matrix products, mm(): return jnp.einsum(spec, a, b, preferred_element_type=f32)  40 us
    psum x1, blocking collectives, attention_backward(): g_state = lax.psum(mm('htm,htd->hmd', q_feat, g_num), 'feat').astype(bf16)  20.8 us
    psum x1, blocking collectives, attention_forward(): state = lax.psum(mm('htm,htd->hmd', k_feat, v), 'feat').astype(bf16)  20.2 us
    unnamed x74, local copies, waits for them, and re-layouts  11.5 us
    reshape x8, local copies, waits for them, and re-layouts, on_device(): p.reshape(shards, -1)  10.4 us
    all_gather x1, blocking collectives, on_device(): features = lax.all_gather(feature_matrix, 'feat', axis=1, tiled=True)  10.3 us
    pmax x1, blocking collectives, attention_forward(): k_top = lax.pmax(jnp.max(k_shift, axis=(1, 2)), 'feat')[:, None, None]  7.3 us

profile of v2, /device:TPU:0, one launch (start us, length us, event | category | flops | bytes accessed | tf_op | source)
XLA Modules:
  0.0 249.4 jit_solution(4766225950911865656)
XLA Ops:
  2.8 2.1 fusion.2
  5.9 1.9 copy.51
  8.9 10.3 %all_gather.3 = bf16[12,256,64]{2,1,0:T(8,128)(2,1)S(1)} all-gather(bf16[12,64,64]{2,1,0:T(8,128)(2,1)} %param.30), channel_id=1, replica_groups=mesh['dp'=8,'feat'=4] {'feat'}, dimensions={1}, use_global_device_ids=true | all-gather | bytes 491520 | tf_op jit(solution)/shard_map/all_gather | solution.py:397
  20.1 3.8 %fusion.9 = (f32[12]{0:T(128)}, f32[12,256,256]{1,2,0:T(8,128)}) fusion(f32[12,256]{1,0:T(8,128)S(1)} %broadcast_multiply_fusion, bf16[12,256,64]{2,1,0:T(8,128)(2,1)S(1)} %all_gather.3, bf16[12,256,64]{1,2,0:T(8,128)(2,1)} %bitcast.87), kind=kOutput, calls=%fused_computation.25 | convolution fusion | flops 103022576 | bytes 3944496 | tf_op jit(solution)/shard_map/htd,hmd->htm/dot_general | solution.py:16
  23.9 7.3 %pmax.7 = f32[12]{0:T(128)} all-reduce(f32[12]{0:T(128)} %get-tuple-element.65), channel_id=1, replica_groups=mesh['dp'=8,'feat'=4] {'feat'}, use_global_device_ids=true, to_apply=%region_4.5 | all-reduce | flops 12 | bytes 96 | tf_op jit(solution)/shard_map/pmax | solution.py:51
  31.2 4.5 %convert_reduce_fusion.1 = (f32[12,256]{1,0:T(8,128)}, bf16[12,256,256]{1,2,0:T(8,128)(2,1)}) fusion(f32[]{:T(128)} %bitcast.6, f32[12]{0:T(128)} %pmax.7, f32[12,256]{1,0:T(8,128)S(1)} %broadcast_multiply_fusion, f32[12,256,256]{1,2,0:T(8,128)} %get-tuple-element.66), kind=kLoop, calls=%fused_computation.20 | loop fusion | flops 5501952 | bytes 4743220 | tf_op jit(solution)/shard_map/reduce_sum | solution.py:56
  35.7 1.9 copy.53
  37.6 2.9 %fusion.68 = f32[12,256,64]{1,2,0:T(8,128)} fusion(bf16[12,256,256]{1,2,0:T(8,128)(2,1)} %get-tuple-element.51, bf16[12,256,64]{1,2,0:T(8,128)(2,1)} %bitcast.98), kind=kOutput, calls=%fused_computation.115 | convolution fusion | flops 100663296 | bytes 2752512 | tf_op jit(solution)/shard_map/htm,htd->hmd/dot_general | solution.py:16
  40.6 20.2 %all-reduce.5 = (bf16[12,256,64]{1,2,0:T(8,128)(2,1)}, f32[12,256]{1,0:T(8,128)}) all-reduce(f32[12,256,64]{1,2,0:T(8,128)} %fusion.68, f32[12,256]{1,0:T(8,128)} %get-tuple-element.50), channel_id=1, replica_groups=mesh['dp'=8,'feat'=4] {'feat'}, use_global_device_ids=true, to_apply=%region_5.6 | all-reduce | flops 199680 | bytes 1204224 | tf_op jit(solution)/shard_map/psum | solution.py:55
  60.7 1.9 copy.50
  64.4 5.4 %fusion.3 = (f32[12,256]{1,0:T(8,128)}, bf16[12,256,256]{1,2,0:T(8,128)(2,1)}, f32[12,256,256]{1,2,0:T(8,128)}) fusion(f32[12,256]{1,0:T(8,128)} %get-tuple-element.36, f32[12,256]{1,0:T(8,128)} %broadcast_multiply_fusion.1, bf16[12,256,64]{2,1,0:T(8,128)(2,1)} %copy-done.1, bf16[12,256,64]{1,2,0:T(8,128)(2,1)} %bitcast.90), kind=kOutput, calls=%fused_computation.9 | convolution fusion | flops 106955008 | bytes 5541888 | tf_op jit(solution)/shard_map/sub | solution.py:52
  70.6 1.9 fusion.43
  72.6 1.2 fusion.62
  74.4 3.7 %multiply_convert_fusion = (bf16[256,3072]{1,0:T(8,128)(2,1)S(1)}, f32[256,3072]{1,0:T(8,128)S(1)}) fusion(f32[3072]{0:T(1024)S(1)} %copy-done.27, bf16[256,768]{1,0:T(8,128)(2,1)S(1)} %fusion.48.refs_2_, bf16[768,3072]{1,0:T(8,128)(2,1)} %param.24), kind=kOutput, calls=%fused_computation.18 | convolution fusion | flops 1212678144 | bytes 9842688 | tf_op jit(solution)/shard_map/td,df->tf/dot_general | solution.py:16
  78.2 2.1 fusion.60
  81.6 1.7 convert_reduce_fusion.3
  83.3 3.0 %convert_reduce_fusion = (f32[3072]{0:T(1024)}, bf16[256,3072]{1,0:T(8,128)(2,1)S(1)}) fusion(f32[256,3072]{1,0:T(8,128)S(1)} %get-tuple-element.71, bf16[256,768]{1,0:T(8,128)(2,1)S(1)} %get-tuple-element.38.refs_7_, bf16[3072,768]{1,0:T(8,128)(2,1)S(1)} %bitcast.108), kind=kOutput, calls=%fused_computation.15 | convolution fusion | flops 1217393664 | bytes 9842688 | tf_op jit(solution)/shard_map/td,fd->tf/dot_general | solution.py:16
  86.3 2.4 multiply_reduce_fusion.3
  88.8 1.8 convert_reduce_fusion.4
  91.8 1.5 fusion.57
  95.2 20.8 %all-reduce.6 = (bf16[12,256,64]{1,2,0:T(8,128)(2,1)}, f32[12,256]{1,0:T(8,128)}) all-reduce(f32[12,256,64]{1,2,0:T(8,128)} %fusion.57, f32[12,256]{1,0:T(8,128)} %fusion.4), channel_id=1, replica_groups=mesh['dp'=8,'feat'=4] {'feat'}, use_global_device_ids=true, to_apply=%region_19.20 | all-reduce | flops 199680 | bytes 1204224 | tf_op jit(solution)/shard_map/psum | solution.py:73
  116.0 2.7 %convolution_convert_fusion = bf16[12,256,64]{1,2,0:T(8,128)(2,1)} fusion(bf16[12,256,256]{1,2,0:T(8,128)(2,1)} %get-tuple-element.51, bf16[12,256,64]{1,2,0:T(8,128)(2,1)} %get-tuple-element.33), kind=kOutput, calls=%fused_computation.48 | convolution fusion | flops 100859904 | bytes 2359296 | tf_op jit(solution)/shard_map/htm,hmd->htd/dot_general | solution.py:16
  118.7 1.9 copy.65
  120.6 3.5 %fusion.66 = (f32[12,256]{1,0:T(8,128)S(1)}, bf16[12,256,256]{1,2,0:T(8,128)(2,1)S(1)}) fusion(f32[]{:T(128)} %bitcast.6, f32[12]{0:T(128)} %pmax.7, f32[12,256]{1,0:T(8,128)S(1)} %broadcast_multiply_fusion, f32[12,256,256]{1,2,0:T(8,128)} %get-tuple-element.66, f32[12,256]{1,0:T(8,128)} %get-tuple-element.34, bf16[12,256,64]{1,2,0:T(8,128)(2,1)} %bitcast.99, ...), kind=kOutput, calls=%fused_computation.113 | convolution fusion | flops 106951680 | bytes 5541940 | tf_op jit(solution)/shard_map/htd,hmd->htm/dot_general | solution.py:16
  125.3 1.9 copy.64
  127.2 3.2 %fusion.67 = (f32[12,256]{1,0:T(8,128)S(1)}, bf16[12,256,256]{1,2,0:T(8,128)(2,1)S(1)}) fusion(f32[12,256,256]{1,2,0:T(8,128)} %get-tuple-element.67, f32[12,256]{1,0:T(8,128)} %get-tuple-element.36, f32[12,256]{1,0:T(8,128)S(1)} %copy-done.20, bf16[12,256,64]{1,2,0:T(8,128)(2,1)} %get-tuple-element.35, f32[12,256,64]{1,2,0:T(8,128)} %bitcast.94, ...), kind=kOutput, calls=%fused_computation.114 | convolution fusion | flops 105182208 | bytes 5947396 | tf_op jit(solution)/shard_map/htd,hmd->htm/dot_general | solution.py:16
  131.6 1.9 copy.63
  133.5 2.0 convert_reduce_fusion.2
  136.6 3.1 %convolution_add_fusion.3 = f32[256,768]{1,0:T(8,128)} fusion(f32[256,768]{1,0:T(8,128)} %get-tuple-element.41, bf16[256,2304]{1,0:T(8,128)(2,1)S(1)} %get-tuple-element.43.refs_4_, bf16[768,2304]{1,0:T(8,128)(2,1)S(1)} %copy-done), kind=kOutput, calls=%fused_computation.43 | convolution fusion | flops 906166272 | bytes 6291456 | tf_op jit(solution)/shard_map/te,de->td/dot_general | solution.py:16
  139.7 1.9 copy.66.refs_1_
  142.4 1.4 reshape.186
  143.8 1.4 reshape.187
  145.1 1.4 reshape.188
  146.5 1.4 reshape.189
  147.9 1.4 reshape.190
  149.2 1.4 reshape.191
  150.6 1.4 reshape.192
  152.0 2.0 maximum_multiply_fusion
  154.6 1.6 concatenate.7
  157.7 78.7 %scatter_gradients.1 = (f32[24,2304]{1,0:T(8,128)}, f32[24,768]{1,0:T(8,128)}, f32[24,3072]{1,0:T(8,128)}, f32[96,768]{1,0:T(8,128)}, f32[8,128]{1,0:T(8,128)}) custom-call(bf16[256,768]{1,0:T(8,128)(2,1)} %refs_0_.1, bf16[256,768]{1,0:T(8,128)(2,1)} %copy.66.refs_1_, bf16[256,768]{1,0:T(8,128)(2,1)} %copy-done.10, bf16[256,3072]{1,0:T(8,128)(2,1)} %copy-done.12, ...), custom_call_target="tpu_custom_call" | custom-call | tf_op jit(solution)/shard_map/scatter_gradients/pallas_call | solution.py:355
  236.4 1.2 slice.44
  237.6 1.5 fusion.65
  239.1 1.3 slice.48
  241.6 1.3 divide_sqrt_fusion
  242.9 1.6 copy.88
  244.5 1.5 copy.89
  246.0 1.7 copy.90
  247.7 1.7 copy.91
  (103 shorter events, 18.7 us)
Async XLA Ops:
  0.6 2.1 copy-start
  19.2 0.9 copy-start.1
  69.8 2.8 %copy-start.15 = (bf16[768,768]{1,0:T(8,128)(2,1)S(1)}, bf16[768,768]{1,0:T(8,128)(2,1)}, u32[]{:S(2)}) copy-start(bf16[768,768]{1,0:T(8,128)(2,1)} %param.20) | copy-start | bytes 3538948
  69.8 2.8 %copy-start.16 = (bf16[256,768]{1,0:T(8,128)(2,1)S(1)}, bf16[256,768]{1,0:T(8,128)(2,1)}, u32[]{:S(2)}) copy-start(bf16[256,768]{1,0:T(8,128)(2,1)} %refs_0_.1) | copy-start | bytes 1179652
  69.8 2.8 %copy-start.28 = (f32[768]{0:T(1024)S(1)}, f32[768]{0:T(1024)}, u32[]{:S(2)}) copy-start(f32[768]{0:T(1024)} %param.21) | copy-start | bytes 9220
  72.6 5.5 %copy-start.17 = (bf16[256,12,64]{0,2,1:T(8,128)(2,1)}, bf16[256,12,64]{0,2,1:T(8,128)(2,1)S(1)}, u32[]{:S(2)}) copy-start(bf16[256,12,64]{0,2,1:T(8,128)(2,1)S(1)} %get-tuple-element.68) | copy-start | bytes 1179652
  72.6 1.5 copy-start.22
  72.6 1.5 copy-start.24
  72.6 1.7 copy-start.27
  74.1 4.0 %slice-start = ((s8[4718592]{0:T(1024)(128)(4,1)}), s8[4194304]{0:T(1024)(128)(4,1)S(1)}, s32[]{:S(2)}) async-start(s8[4718592]{0:T(1024)(128)(4,1)} %bitcast.107), calls=%async_computation | async-start | bytes 8388608
  74.3 3.8 %copy-start.10 = (bf16[256,768]{1,0:T(8,128)(2,1)}, bf16[256,768]{1,0:T(8,128)(2,1)S(1)}, u32[]{:S(2)}) copy-start(bf16[256,768]{1,0:T(8,128)(2,1)S(1)} %fusion.48.refs_2_) | copy-start | bytes 1179652
  74.4 3.8 %slice-start.1 = ((s8[4718592]{0:T(1024)(128)(4,1)}), s8[524288]{0:T(1024)(128)(4,1)S(1)}, s32[]{:S(2)}) async-start(s8[4718592]{0:T(1024)(128)(4,1)} %bitcast.107), calls=%async_computation.1 | async-start | bytes 1048576
  74.4 3.8 %copy-start.29 = (f32[768]{0:T(1024)S(1)}, f32[768]{0:T(1024)}, u32[]{:S(2)}) copy-start(f32[768]{0:T(1024)} %param.27) | copy-start | bytes 9220
  78.1 2.2 copy-start.12
  78.2 2.4 copy-start.14
  78.2 2.4 copy-start.21
  78.2 3.4 %copy-start.25 = (f32[768]{0:T(1024)S(1)}, f32[768]{0:T(1024)}, u32[]{:S(2)}) copy-start(f32[768]{0:T(1024)} %param.29) | copy-start | bytes 9220
  81.6 4.7 %slice-start.2 = ((s8[4718592]{0:T(1024)(128)(4,1)}), s8[4194304]{0:T(1024)(128)(4,1)S(1)}, s32[]{:S(2)}) async-start(s8[4718592]{0:T(1024)(128)(4,1)} %bitcast.109), calls=%async_computation.2 | async-start | bytes 8388608
  83.3 3.0 %copy-start.11 = (bf16[256,768]{1,0:T(8,128)(2,1)}, bf16[256,768]{1,0:T(8,128)(2,1)S(1)}, u32[]{:S(2)}) copy-start(bf16[256,768]{1,0:T(8,128)(2,1)S(1)} %get-tuple-element.38.refs_7_) | copy-start | bytes 1179652
  83.3 3.0 %slice-start.3 = ((s8[4718592]{0:T(1024)(128)(4,1)}), s8[524288]{0:T(1024)(128)(4,1)S(1)}, s32[]{:S(2)}) async-start(s8[4718592]{0:T(1024)(128)(4,1)} %bitcast.109), calls=%async_computation.3 | async-start | bytes 1048576
  86.3 2.4 copy-start.13
  88.7 3.1 %copy-start.18 = (f32[12,256]{1,0:T(8,128)S(1)}, f32[12,256]{1,0:T(8,128)}, u32[]{:S(2)}) copy-start(f32[12,256]{1,0:T(8,128)} %get-tuple-element.48) | copy-start | bytes 36868
  88.7 3.1 %copy-start.9 = (bf16[12,256,256]{1,2,0:T(8,128)(2,1)S(1)}, bf16[12,256,256]{1,2,0:T(8,128)(2,1)}, u32[]{:S(2)}) copy-start(bf16[12,256,256]{1,2,0:T(8,128)(2,1)} %get-tuple-element.49) | copy-start | bytes 4718596
  90.5 0.7 copy-start.7
  91.8 1.6 copy-start.8
  91.8 1.5 copy-start.23
  93.5 0.6 copy-start.19
  120.6 3.5 %copy-start.2 = (bf16[12,256,64]{2,1,0:T(8,128)(2,1)S(1)}, bf16[12,256,64]{2,1,0:T(8,128)(2,1)}, u32[]{:S(2)}) copy-start(bf16[12,256,64]{2,1,0:T(8,128)(2,1)} %copy-done.1) | copy-start | bytes 1179652
  120.6 3.5 %copy-start.4 = (bf16[256,768]{0,1:T(8,128)(2,1)S(1)}, bf16[256,768]{0,1:T(8,128)(2,1)}, u32[]{:S(2)}) copy-start(bf16[256,768]{0,1:T(8,128)(2,1)} %copy.51) | copy-start | bytes 1179652
  124.1 3.1 %copy-start.20 = (f32[12,256]{1,0:T(8,128)S(1)}, f32[12,256]{1,0:T(8,128)}, u32[]{:S(2)}) copy-start(f32[12,256]{1,0:T(8,128)} %copy-done.19) | copy-start | bytes 36868
  127.2 3.2 %copy-start.3 = (bf16[12,256,64]{2,1,0:T(8,128)(2,1)S(1)}, bf16[12,256,64]{2,1,0:T(8,128)(2,1)}, u32[]{:S(2)}) copy-start(bf16[12,256,64]{2,1,0:T(8,128)(2,1)} %copy-done.1) | copy-start | bytes 1179652
  127.2 3.2 %copy-start.6 = (bf16[256,768]{0,1:T(8,128)(2,1)S(1)}, bf16[256,768]{0,1:T(8,128)(2,1)}, u32[]{:S(2)}) copy-start(bf16[256,768]{0,1:T(8,128)(2,1)} %copy.50) | copy-start | bytes 1179652
  135.5 1.0 copy-start.5
  157.7 82.7 %copy-start.26 = (s32[8,2]{0,1:T(2,128)S(1)}, s32[8,2]{0,1:T(2,128)}, u32[]{:S(2)}) copy-start(s32[8,2]{0,1:T(2,128)} %param.17) | copy-start | bytes 196

commit v3 on v2

--- a/solution.py
+++ b/solution.py
@@ -108,13 +108,18 @@
 
 
 def scatter_kernel(chips, model, *refs):
-    (tok, att, hid, act, g_qkv, g_branch, g_pre, g_ffn, small) = refs[:9]
-    outs = dict(zip(("joint", "output", "up", "down", "small"), refs[9:14]))
-    scratch = list(refs[14:])
-    pair = dict(zip(("tok", "att", "hid", "act", "qkv", "branch", "pre", "ffn", "small"), scratch[:9]))
-    parts = dict(zip(("up", "down", "output", "joint", "small"), scratch[9:14]))
-    pair_send, pair_recv, send, recv = scratch[14:18]
-    rest = scratch[18:]
+    (tok, att, hid, act, g_branch, g_pre, g_ffn) = refs[:7]
+    (qkv, phi_q, phi_k, state, totals, safe, feats, joint_weight, output_weight, g_first) = refs[7:17]
+    row_sums = refs[17:25]
+    outs = dict(zip(("joint", "output", "up", "down", "small", "moments", "input"), refs[25:32]))
+    scratch = list(refs[32:])
+    pair = dict(zip(("tok", "att", "hid", "act", "qkv", "branch", "pre", "ffn"), scratch[:8]))
+    parts = dict(zip(("up", "down", "output", "joint"), scratch[8:12]))
+    pair_send, pair_recv, send, recv, small_send, small_recv = scratch[12:18]
+    sums, near_sums, far_sums = scratch[18:21]
+    (g_qkv, g_att, g_part, near_part, g_sum, far_part, g_state, g_totals, g_totals_parts) = scratch[21:30]
+    state_send, state_recv = scratch[30:32]
+    rest = scratch[32:]
 
     dp, feat = lax.axis_index("dp"), lax.axis_index("feat")
     depth = chips // 4
@@ -129,13 +134,15 @@
             (z * 2 + x + turn * (1 - 2 * x), (y + (1 - turn) * (1 - 2 * y)) * 2 + c),
         )
 
-    routes = {False: route(c), True: route(0)}
+    (p, step_p), (s, step_s), first, second = route(c)
 
     def along(k):
         return ((z + k) % depth * 2 + x, feat)
 
     barrier = pltpu.get_barrier_semaphore()
-    greeted = [core, *routes[False][2:]] + [along(k) for k in range(1, depth)]
+    greeted = [core, first, second] + [along(k) for k in range(1, depth)]
+    far_feat, cross_feat = (1 - y) * 2 + c, (1 - y) * 2 + 1 - c
+    greeted.append((dp, cross_feat))
     for device in greeted:
         pl.semaphore_signal(barrier, inc=1, device_id=device, device_id_type=MESH)
     pl.semaphore_wait(barrier, len(greeted))
@@ -144,9 +151,7 @@
         width = ref.shape[1] // 2
         return ref.at[:, pl.ds(pl.multiple_of((1 - c) * width, 128), width)]
 
-    exchange = []
     sources = (
-        ("small", small.at[:, 1 - c]),
         ("hid", hid),
         ("pre", halves(g_pre)),
         ("ffn", halves(g_ffn)),
@@ -157,17 +162,22 @@
         ("qkv", halves(g_qkv)),
     )
     arrived = {}
-    for i, (name, source) in enumerate(sources):
-        copy = pltpu.make_async_remote_copy(
-            src_ref=source,
-            dst_ref=pair[name],
-            send_sem=pair_send.at[i],
-            recv_sem=pair_recv.at[i],
-            device_id=core,
-            device_id_type=MESH,
-        )
-        copy.start()
-        arrived[name] = copy
+
+    def swap(names):
+        for i, (name, source) in enumerate(sources):
+            if name in names:
+                copy = pltpu.make_async_remote_copy(
+                    src_ref=source,
+                    dst_ref=pair[name],
+                    send_sem=pair_send.at[i],
+                    recv_sem=pair_recv.at[i],
+                    device_id=core,
+                    device_id_type=MESH,
+                )
+                copy.start()
+                arrived[name] = copy
+
+    swap(("hid", "pre", "ffn", "act", "att", "branch", "tok"))
 
     factors = {
         "up": (hid, "hid", g_pre, "pre"),
@@ -177,9 +187,8 @@
     }
 
     chunks = []
-    todo = [("small", 128, 1)] + list(plan(model, g_qkv.shape[1], g_pre.shape[1]))
     at = 0
-    for name, w, count in todo:
+    for name, w, count in plan(model, g_qkv.shape[1], g_pre.shape[1]):
         for k in range(count):
             part = parts[name]
             r = part.shape[0] // chips
@@ -206,7 +215,6 @@
             parts[name][rows, columns : columns + w] = total.astype(bf16)
 
     def block(chunk, zb, pb, sb):
-        (_, step_p), (_, step_s), _, _ = routes[chunk.kind == "small"]
         q = 4 * zb + step_p * pb + step_s * sb
         rows = pl.ds(pl.multiple_of(q * chunk.r, min(chunk.r, 16)), chunk.r)
         return chunk.part.at[rows, pl.ds(chunk.first, chunk.w)]
@@ -224,29 +232,20 @@
     def done(sems, chunk, stage, ref):
         pltpu.make_async_copy(ref, ref, sems.at[chunk.sems, stage]).wait()
 
-    def places(chunk):
-        (p, _), (s, _), first, second = routes[chunk.kind == "small"]
-        return p, s, first, second
-
     made = set()
 
     def stage_0(chunk):
-        if chunk.kind == "small":
-            arrived.pop("small").wait_recv()
-            chunk.part[...] = (small[:, c] + pair["small"][...]).reshape(chunk.part.shape)
-        elif chunk.kind == "down":
+        if chunk.kind == "down":
             if "down" not in made:
                 made.add("down")
                 product("down", 0, chunk.part.shape[1])
         else:
             product(chunk.kind, chunk.first, chunk.w)
-        p, _, first, _ = places(chunk)
         for zb in range(depth):
             for sb in range(2):
                 start(block(chunk, zb, 1 - p, sb), chunk.b1.at[2 * zb + sb], chunk, 0, first)
 
     def stage_1(chunk):
-        p, s, _, second = places(chunk)
         done(recv, chunk, 0, chunk.b1)
         for zb in range(depth):
             for sb in range(2):
@@ -257,7 +256,6 @@
             start(chunk.b1.at[2 * zb + 1 - s], chunk.b2.at[zb], chunk, 1, second)
 
     def stage_2(chunk):
-        _, s, _, _ = places(chunk)
         done(recv, chunk, 1, chunk.b2)
         for zb in range(depth):
             total = chunk.b2[zb].astype(f32) + chunk.b1[2 * zb + s].astype(f32)
@@ -271,16 +269,11 @@
         total = chunk.b3[0].astype(f32)
         for k in range(1, depth):
             total += chunk.b3[k].astype(f32)
-        if chunk.kind == "small":
-            outs["small"][...] = total
-            return
         chunk.fin[...] = total
         half = chunk.r // 2
         start(chunk.fin.at[pl.ds(pl.multiple_of((1 - c) * half, 8), half)], chunk.got, chunk, 3, core)
 
     def stage_4(chunk):
-        if chunk.kind == "small":
-            return
         done(recv, chunk, 3, chunk.got)
         out = outs[chunk.kind]
         width = out.shape[1] // 2
@@ -291,12 +284,206 @@
 
         out[:, columns(c)] = chunk.fin[pl.ds(pl.multiple_of(c * half, 8), half), :]
         out[:, columns(1 - c)] = chunk.got[...]
+
+    _, _, along_x, along_y = route(0)
+
+    def small_step(k):
+        if k == 0:
+            sums[0] = jnp.zeros(sums.shape[1:], f32)
+            sums[0, 0:1, 0 : g_qkv.shape[1]] = jnp.sum(
+                g_qkv[...].astype(f32), axis=0, keepdims=True
+            )
+            for i, source in enumerate(row_sums[:7]):
+                sums[0, i + 1 : i + 2, 0 : source.shape[1]] = source[...]
+            sums[0, 1:2, sums.shape[2] - 128 :] = row_sums[7][...]
+        elif k < 4:
+            arrive = pltpu.make_async_copy(near_sums.at[k - 1], near_sums.at[k - 1], small_recv.at[k - 1])
+            arrive.wait()
+            sums[k] = sums[k - 1] + near_sums[k - 1]
+        if k < 3:
+            targets = [(near_sums.at[k], (core, along_x, along_y)[k])]
+        elif k == 3:
+            targets = [(far_sums.at[z], along(j)) for j in range(1, depth)]
+        else:
+            waited = far_sums.at[pl.ds(0, depth - 1)]
+            pltpu.make_async_copy(waited, waited, small_recv.at[3]).wait()
+            total = far_sums[0]
+            for j in range(1, depth):
+                total += far_sums[j]
+            outs["moments"][...] = total[:, total.shape[1] - 128 :]
+            width = total.shape[1]
+            place = dp * 4 + feat
+            turned = {}
+            for i, source in enumerate((g_qkv, *row_sums[:7])):
+                own = source.shape[1] // (2 * chips)
+                if own not in turned:
+                    turned[own] = pltpu.roll(total, (width - own * place) % width, 1)[:, :128]
+                outs["small"][i : i + 1, :] = turned[own][i : i + 1, :]
+            return
+        for target, device in targets:
+            pltpu.make_async_remote_copy(
+                src_ref=sums.at[k],
+                dst_ref=target,
+                send_sem=small_send.at[k],
+                recv_sem=small_recv.at[k],
+                device_id=device,
+                device_id_type=MESH,
+            ).start()
+        if k == 3:
+            far_sums[z] = sums[3]
+
+    rows = tok.shape[0]
+    pairs, count, lanes = feats.shape
+    size = lanes // 2
+    scale = size ** (-0.25)
+    half = pairs // 2
+    mine, theirs = c * half, (1 - c) * half
+    lane = lax.broadcasted_iota(jnp.int32, (rows, lanes), 1)
+    state_row = lax.broadcasted_iota(jnp.int32, (lanes, count), 0)
+
+    def own_half(value, b):
+        return jnp.where(lane // size == b, value, jnp.zeros_like(value))
+
+    def either(values):
+        return jnp.where(lane < size, values[0], values[1])
+
+    def of_head(h):
+        return pl.ds(pl.multiple_of(h * count, count), count)
+
+    def of_pair(base, i):
+        return pl.ds(pl.multiple_of(base * model + i * lanes, lanes), lanes)
+
+    def to_inputs(grads, base, i):
+        inputs = qkv[:, of_pair(base, i)].astype(f32)
+        results = []
+        for grad in grads:
+            linear = scale * jnp.dot(grad.astype(bf16), feats[i], preferred_element_type=f32)
+            results.append(linear - scale * scale * inputs * jnp.sum(grad, -1, keepdims=True))
+        g_qkv[:, of_pair(base, i)] = either(results).astype(bf16)
+
+    def query_back(i):
+        grad = g_att[:, of_pair(0, i)]
+        ratio = grad * att[:, of_pair(0, i)].astype(f32)
+        tops, dens = [], []
+        for b in range(2):
+            top = 1.0 / jnp.sum(jnp.where(lane == 2 * i + b, safe[...], 0.0), -1, keepdims=True)
+            tops.append(top)
+            den = -jnp.sum(own_half(ratio, b), -1, keepdims=True) * top
+            dens.append(den.astype(bf16).astype(f32))
+        numer = (grad * either(tops)).astype(bf16)
+        products, logits = [], []
+        for b in range(2):
+            h = 2 * i + b
+            low = phi_q[:, of_head(h)]
+            wide = low.astype(f32)
+            products.append(dot(numer, low, 0, 0))
+            g_totals_parts[feat, pl.ds(h, 1), :] = jnp.sum(wide * dens[b], axis=0, keepdims=True)
+            back = jnp.dot(own_half(numer, b), state[i], preferred_element_type=f32)
+            logits.append((back + dens[b] * totals[pl.ds(h, 1), :]) * wide)
+        g_part[i] = jnp.where(state_row < size, products[0], products[1]).astype(bf16)
+        to_inputs(logits, 0, i)
+
+    def key_back(i):
+        values = qkv[:, of_pair(2, i)]
+        held = g_state[i]
+        logits, g_values = [], []
+        for b in range(2):
+            h = 2 * i + b
+            low = phi_k[:, of_head(h)]
+            back = jnp.dot(own_half(values, b), held, preferred_element_type=f32)
+            logits.append((back + g_totals[pl.ds(h, 1), :]) * low.astype(f32))
+            g_values.append(dot(low, held, 1, 1))
+        g_qkv[:, of_pair(2, i)] = either(g_values).astype(bf16)
+        to_inputs(logits, 1, i)
+
+    def state_copy(source, target, i, other):
+        copy = pltpu.make_async_remote_copy(
+            src_ref=source,
+            dst_ref=target,
+            send_sem=state_send.at[i],
+            recv_sem=state_recv.at[i],
+            device_id=(dp, other),
+            device_id_type=MESH,
+        )
+        copy.start()
+        return copy
+
+    moved = {}
+
+    def attention_a():
+        g_totals_parts[feat] = jnp.zeros(g_totals_parts.shape[1:], f32)
+        tile = 256
+
+        @pl.loop(0, model // tile)
+        def _(i):
+            own = pl.ds(pl.multiple_of(i * tile, tile), tile)
+            g_att[:, own] = dot(g_branch[...], output_weight[own, :], 1, 1)
+
+        @pl.loop(0, half)
+        def _(j):
+            query_back(theirs + j)
+
+        moved["near"] = state_copy(g_part.at[pl.ds(theirs, half)], near_part, 0, y * 2 + 1 - c)
+
+    def attention_b():
+        @pl.loop(0, half)
+        def _(j):
+            query_back(mine + j)
+
+        for other in (y * 2 + 1 - c, far_feat, cross_feat):
+            state_copy(g_totals_parts.at[feat], g_totals_parts.at[feat], 1, other)
+        moved["near"].wait_recv()
+        g_sum[...] = (g_part[pl.ds(mine, half)].astype(f32) + near_part[...].astype(f32)).astype(bf16)
+        moved["far"] = state_copy(g_sum, far_part, 2, far_feat)
+
+    three_totals = g_totals_parts.at[pl.ds(0, 3)]
+
+    def attention_c():
+        moved["far"].wait_recv()
+        own = pl.ds(mine, half)
+        g_state[own] = (g_sum[...].astype(f32) + far_part[...].astype(f32)).astype(bf16)
+        moved["back"] = state_copy(g_state.at[own], g_state.at[own], 3, y * 2 + 1 - c)
+        pltpu.make_async_copy(three_totals, three_totals, state_recv.at[1]).wait()
+        g_totals[...] = (g_totals_parts[0] + g_totals_parts[1]) + (g_totals_parts[2] + g_totals_parts[3])
+
+        @pl.loop(0, half)
+        def _(j):
+            key_back(mine + j)
+
+    def attention_d():
+        moved["back"].wait_recv()
+
+        @pl.loop(0, half)
+        def _(j):
+            key_back(theirs + j)
+
+        swap(("qkv",))
+
+    def attention_e():
+        tile = 256
+
+        @pl.loop(0, model // tile)
+        def _(i):
+            own = pl.ds(pl.multiple_of(i * tile, tile), tile)
+            outs["input"][:, own] = g_first[:, own] + dot(g_qkv[...], joint_weight[own, :], 1, 1)
+
+    attention_steps = {
+        0: attention_a,
+        1: attention_b,
+        3: attention_c,
+        4: attention_d,
+        5: attention_e,
+    }
 
     stages = ((stage_0, 0), (stage_1, 2), (stage_2, 3), (stage_3, 4), (stage_4, 5))
     for step in range(len(chunks) + 5):
         for stage, lag in stages:
             if 0 <= step - lag < len(chunks):
                 stage(chunks[step - lag])
+        if 7 <= step <= 11:
+            small_step(step - 7)
+        if step in attention_steps:
+            attention_steps[step]()
 
     for i, (name, source) in enumerate(sources):
         pltpu.make_async_copy(pair[name], pair[name], pair_send.at[i]).wait()
@@ -304,13 +491,21 @@
         done(send, chunk, 0, chunk.b1)
         done(send, chunk, 1, chunk.b2)
         done(send, chunk, 2, chunk.b3.at[pl.ds(0, depth - 1)])
-        if chunk.kind != "small":
-            done(send, chunk, 3, chunk.got)
-
-
-def scatter_gradients(chips, tok, att, hid, act, g_qkv, g_branch, g_pre, g_ffn, small):
+        done(send, chunk, 3, chunk.got)
+    for made in moved.values():
+        made.wait_send()
+    pltpu.make_async_copy(three_totals, three_totals, state_send.at[1]).wait()
+    for i in range(3):
+        pltpu.make_async_copy(near_sums.at[i], near_sums.at[i], small_send.at[i]).wait()
+    waited = far_sums.at[pl.ds(0, depth - 1)]
+    pltpu.make_async_copy(waited, waited, small_send.at[3]).wait()
+
+
+def scatter_gradients(chips, tok, att, hid, act, g_branch, g_pre, g_ffn, saved, weights, g_first, row_sums):
     rows, model = tok.shape
     devices = 2 * chips
+    g_qkv, feats = saved[0], saved[-1]
+    pairs, features, lanes = feats.shape
     joint, up = g_qkv.shape[1], g_pre.shape[1]
     halved = {"qkv": joint // 2, "branch": model // 2, "pre": up // 2, "ffn": model // 2}
     scratch = [
@@ -322,25 +517,41 @@
         pltpu.VMEM((rows, halved["branch"]), bf16),
         pltpu.VMEM((rows, halved["pre"]), bf16),
         pltpu.VMEM((rows, halved["ffn"]), bf16),
-        pltpu.VMEM((chips, 8, 128), f32),
     ]
     sizes = {
         "up": (model, up // 2, bf16),
         "down": (up, model // 2, bf16),
         "output": (model, model // 2, bf16),
         "joint": (model, joint // 2, bf16),
-        "small": (chips * 8, 128, f32),
     }
-    scratch += [pltpu.VMEM(sizes[k][:2], sizes[k][2]) for k in ("up", "down", "output", "joint", "small")]
-    todo = [("small", 128, 1)] + list(plan(model, joint, up))
+    scratch += [pltpu.VMEM(sizes[k][:2], sizes[k][2]) for k in ("up", "down", "output", "joint")]
+    todo = plan(model, joint, up)
     count = sum(n for _, _, n in todo)
     scratch += [
-        pltpu.SemaphoreType.DMA((9,)),
-        pltpu.SemaphoreType.DMA((9,)),
+        pltpu.SemaphoreType.DMA((8,)),
+        pltpu.SemaphoreType.DMA((8,)),
         pltpu.SemaphoreType.DMA((count, 4)),
         pltpu.SemaphoreType.DMA((count, 4)),
+        pltpu.SemaphoreType.DMA((4,)),
+        pltpu.SemaphoreType.DMA((4,)),
     ]
     depth = chips // 4
+    scratch += [
+        pltpu.VMEM((4, 8, up), f32),
+        pltpu.VMEM((3, 8, up), f32),
+        pltpu.VMEM((depth, 8, up), f32),
+        pltpu.VMEM((rows, joint), bf16),
+        pltpu.VMEM((rows, model), f32),
+        pltpu.VMEM((pairs, lanes, features), bf16),
+        pltpu.VMEM((pairs // 2, lanes, features), bf16),
+        pltpu.VMEM((pairs // 2, lanes, features), bf16),
+        pltpu.VMEM((pairs // 2, lanes, features), bf16),
+        pltpu.VMEM((pairs, lanes, features), bf16),
+        pltpu.VMEM((16, features), f32),
+        pltpu.VMEM((4, 16, features), f32),
+        pltpu.SemaphoreType.DMA((4,)),
+        pltpu.SemaphoreType.DMA((4,)),
+    ]
     for name, w, n in todo:
         r, kind = sizes[name][0] // chips, sizes[name][2]
         for _ in range(n):
@@ -349,7 +560,7 @@
                 pltpu.VMEM((depth, r, w), kind),
                 pltpu.VMEM((depth, r, w), kind),
                 pltpu.VMEM((r, w), f32),
-                pltpu.VMEM((max(r // 2, 8), w), f32),
+                pltpu.VMEM((r // 2, w), f32),
             ]
     vmem = pl.BlockSpec(memory_space=pltpu.VMEM)
     return pl.pallas_call(
@@ -360,15 +571,251 @@
             jax.ShapeDtypeStruct((model // devices, up), f32),
             jax.ShapeDtypeStruct((up // devices, model), f32),
             jax.ShapeDtypeStruct((8, 128), f32),
+            jax.ShapeDtypeStruct((8, 128), f32),
+            jax.ShapeDtypeStruct((rows, model), f32),
         ),
-        in_specs=[vmem] * 9,
-        out_specs=(vmem,) * 5,
+        in_specs=[vmem] * 25,
+        out_specs=(vmem,) * 7,
         scratch_shapes=scratch,
         compiler_params=pltpu.CompilerParams(
             collective_id=0, has_side_effects=True, vmem_limit_bytes=60 << 20
         ),
         name="scatter_gradients",
-    )(tok, att, hid, act, g_qkv, g_branch, g_pre, g_ffn, small)
+    )(tok, att, hid, act, g_branch, g_pre, g_ffn, *saved, *weights, g_first, *row_sums)
+
+
+def dot(a, b, left, right):
+    return lax.dot_general(a, b, (((left,), (right,)), ((), ())), preferred_element_type=f32)
+
+
+def attention_kernel(*refs):
+    (tok, weight, bias, shard, valid_ref) = refs[:5]
+    (att, qkv, phi_q, phi_k, state, totals, safe, kept) = refs[5:13]
+    (feats, shift, tops, part, pair_part, pair_sum, far_sum, part_totals) = refs[13:21]
+    send, recv = refs[21:23]
+    rows, model = tok.shape
+    pairs, share, lanes = shard.shape
+    size = lanes // 2
+    count = feats.shape[1]
+    heads = 2 * pairs
+    scale = size ** (-0.25)
+    norm = count ** (-0.5)
+    dp, feat = lax.axis_index("dp"), lax.axis_index("feat")
+    y, c = feat // 2, feat % 2
+    core, far, cross = y * 2 + 1 - c, (1 - y) * 2 + c, (1 - y) * 2 + 1 - c
+    others = (core, far, cross)
+
+    barrier = pltpu.get_barrier_semaphore()
+    for other in others:
+        pl.semaphore_signal(barrier, inc=1, device_id=(dp, other), device_id_type=MESH)
+    pl.semaphore_wait(barrier, 3)
+
+    def copy(source, target, i, other):
+        made = pltpu.make_async_remote_copy(
+            src_ref=source,
+            dst_ref=target,
+            send_sem=send.at[i],
+            recv_sem=recv.at[i],
+            device_id=(dp, other),
+            device_id_type=MESH,
+        )
+        made.start()
+        return made
+
+    def slot(owner):
+        return feats.at[:, pl.ds(pl.multiple_of(owner * share, share), share), :]
+
+    to_far = copy(shard, slot(feat), 0, far)
+    to_core = copy(shard, slot(feat), 1, core)
+    feats[:, pl.ds(pl.multiple_of(feat * share, share), share), :] = shard[...]
+
+    tile = 256
+
+    @pl.loop(0, qkv.shape[1] // tile)
+    def _(i):
+        columns = pl.ds(pl.multiple_of(i * tile, tile), tile)
+        total = jnp.dot(tok[...], weight[:, columns], preferred_element_type=f32)
+        qkv[:, columns] = (total + bias[:, columns]).astype(bf16)
+
+    to_far.wait_recv()
+    passed = copy(slot(far), slot(far), 2, core)
+    to_core.wait_recv()
+    passed.wait_recv()
+
+    lane = lax.broadcasted_iota(jnp.int32, (rows, lanes), 1)
+    row_lane = lax.broadcasted_iota(jnp.int32, (8, 128), 1)
+
+    def pair_of(base, i):
+        return qkv[:, pl.ds(pl.multiple_of(base * model + i * lanes, lanes), lanes)]
+
+    def own_half(value, b):
+        return jnp.where(lane // size == b, value, jnp.zeros_like(value))
+
+    def of_head(h):
+        return pl.ds(pl.multiple_of(h * count, count), count)
+
+    def key_logits(i, top):
+        keys = pair_of(1, i)
+        for b in range(2):
+            mine = own_half(keys, b)
+            wide = mine.astype(f32)
+            logits = scale * dot(mine, feats[i], 1, 1) - (
+                scale * scale / 2 * jnp.sum(wide * wide, -1, keepdims=True)
+            )
+            shift[2 * i + b] = logits
+            best = jnp.max(jnp.max(logits, axis=1, keepdims=True), axis=0, keepdims=True)
+            top = jnp.where(row_lane == 2 * i + b, best, top)
+        return top
+
+    tops[feat] = lax.fori_loop(0, pairs, key_logits, jnp.full((8, 128), -1e30, f32))
+    top_copies = [copy(tops.at[feat], tops.at[feat], 3, other) for other in others]
+
+    @pl.loop(0, pairs)
+    def _(i):
+        queries = pair_of(0, i)
+        for b in range(2):
+            logits = scale * dot(own_half(queries, b), feats[i], 1, 1)
+            raw = jnp.exp(logits - jnp.max(logits, -1, keepdims=True)) * norm
+            phi_q[:, of_head(2 * i + b)] = raw.astype(bf16)
+
+    three = tops.at[pl.ds(0, 3)]
+    pltpu.make_async_copy(three, three, recv.at[3]).wait()
+    top = jnp.maximum(jnp.maximum(tops[0], tops[1]), jnp.maximum(tops[2], tops[3]))
+    valid = valid_ref[0, 0]
+    state_row = lax.broadcasted_iota(jnp.int32, (lanes, count), 0)
+    part_totals[feat] = jnp.zeros(part_totals.shape[1:], f32)
+
+    def key_state(i):
+        values = pair_of(2, i)
+        products = []
+        for b in range(2):
+            h = 2 * i + b
+            best = jnp.max(jnp.where(row_lane == h, top, -1e30), axis=1, keepdims=True)[:1]
+            raw = (jnp.exp(shift[h] - best) * (norm * valid)).astype(bf16)
+            phi_k[:, of_head(h)] = raw
+            part_totals[feat, pl.ds(h, 1), :] = jnp.sum(raw.astype(f32), axis=0, keepdims=True)
+            products.append(dot(values, raw, 0, 0))
+        part[i] = jnp.where(state_row < size, products[0], products[1]).astype(bf16)
+
+    half = pairs // 2
+    mine, theirs = c * half, (1 - c) * half
+
+    @pl.loop(0, half)
+    def _(j):
+        key_state(theirs + j)
+
+    near = copy(part.at[pl.ds(theirs, half)], pair_part, 4, core)
+
+    @pl.loop(0, half)
+    def _(j):
+        key_state(mine + j)
+
+    for other in others:
+        copy(part_totals.at[feat], part_totals.at[feat], 5, other)
+    near.wait_recv()
+    pair_sum[...] = (part[pl.ds(mine, half)].astype(f32) + pair_part[...].astype(f32)).astype(bf16)
+    across = copy(pair_sum, far_sum, 6, far)
+    across.wait_recv()
+    state[pl.ds(mine, half)] = (pair_sum[...].astype(f32) + far_sum[...].astype(f32)).astype(bf16)
+    back = copy(state.at[pl.ds(mine, half)], state.at[pl.ds(mine, half)], 7, core)
+    three_totals = part_totals.at[pl.ds(0, 3)]
+    pltpu.make_async_copy(three_totals, three_totals, recv.at[5]).wait()
+    totals[...] = (part_totals[0] + part_totals[1]) + (part_totals[2] + part_totals[3])
+    safe[...] = jnp.ones(safe.shape, f32)
+
+    def attend(i):
+        held = state[i]
+        results = []
+        for b in range(2):
+            h = 2 * i + b
+            feature = phi_q[:, of_head(h)]
+            denom = jnp.sum(feature.astype(f32) * totals[pl.ds(h, 1), :], -1, keepdims=True)
+            bottom = denom + (1.0 - valid)
+            safe[...] = jnp.where(
+                lax.broadcasted_iota(jnp.int32, safe.shape, 1) == h, bottom, safe[...]
+            )
+            results.append(dot(feature, held, 1, 1) / bottom)
+        att[:, pl.ds(pl.multiple_of(i * lanes, lanes), lanes)] = jnp.where(
+            lane < size, results[0], results[1]
+        ).astype(bf16)
+
+    @pl.loop(0, half)
+    def _(j):
+        attend(mine + j)
+
+    back.wait_recv()
+
+    @pl.loop(0, half)
+    def _(j):
+        attend(theirs + j)
+
+    kept[...] = feats[...]
+    for made in (to_far, to_core, passed, near, across, back):
+        made.wait_send()
+    pltpu.make_async_copy(three, three, send.at[3]).wait()
+    pltpu.make_async_copy(three_totals, three_totals, send.at[5]).wait()
+
+
+def attention_call(tokens, weight, bias, features, valid):
+    rows, model = tokens.shape
+    heads, share, size = features.shape
+    count = share * 4
+    pairs, lanes = heads // 2, 2 * size
+    shard = features.reshape(pairs, 2, share, size).transpose(0, 2, 1, 3).reshape(pairs, share, lanes)
+    vmem = pl.BlockSpec(memory_space=pltpu.VMEM)
+    return pl.pallas_call(
+        attention_kernel,
+        out_shape=(
+            jax.ShapeDtypeStruct((rows, model), bf16),
+            jax.ShapeDtypeStruct((rows, 3 * model), bf16),
+            jax.ShapeDtypeStruct((rows, heads * count), bf16),
+            jax.ShapeDtypeStruct((rows, heads * count), bf16),
+            jax.ShapeDtypeStruct((pairs, lanes, count), bf16),
+            jax.ShapeDtypeStruct((16, count), f32),
+            jax.ShapeDtypeStruct((rows, 128), f32),
+            jax.ShapeDtypeStruct((pairs, count, lanes), bf16),
+        ),
+        in_specs=[vmem] * 4 + [pl.BlockSpec(memory_space=pltpu.SMEM)],
+        out_specs=(vmem,) * 8,
+        scratch_shapes=[
+            pltpu.VMEM((pairs, count, lanes), bf16),
+            pltpu.VMEM((heads, rows, count), f32),
+            pltpu.VMEM((4, 8, 128), f32),
+            pltpu.VMEM((pairs, lanes, count), bf16),
+            pltpu.VMEM((pairs // 2, lanes, count), bf16),
+            pltpu.VMEM((pairs // 2, lanes, count), bf16),
+            pltpu.VMEM((pairs // 2, lanes, count), bf16),
+            pltpu.VMEM((4, 16, count), f32),
+            pltpu.SemaphoreType.DMA((8,)),
+            pltpu.SemaphoreType.DMA((8,)),
+        ],
+        compiler_params=pltpu.CompilerParams(
+            collective_id=1, has_side_effects=True, vmem_limit_bytes=40 << 20
+        ),
+        name="attention",
+    )(tokens, weight, bias.reshape(1, -1), shard, valid.reshape(1, 1))
+
+
+def finish_kernel(*refs):
+    (count, joint, output, up, down, inputs, small, moments) = refs[:8]
+    outs = refs[8:]
+    for source, target in zip((joint, output, up, down, inputs), outs[:5]):
+        target[...] = source[...]
+    for i, target in enumerate(outs[5:13]):
+        target[...] = small[i, 0 : target.shape[0]]
+    outs[13][...] = jnp.sqrt(moments[1, 0:3] / count[0, 0])
+
+
+def finish(count, big, small, moments, widths):
+    vmem = pl.BlockSpec(memory_space=pltpu.VMEM)
+    return pl.pallas_call(
+        finish_kernel,
+        out_shape=tuple(jax.ShapeDtypeStruct(b.shape, f32) for b in big)
+        + tuple(jax.ShapeDtypeStruct((w,), f32) for w in widths),
+        in_specs=[pl.BlockSpec(memory_space=pltpu.SMEM)] + [vmem] * 7,
+        out_specs=(vmem,) * 14,
+        name="finish",
+    )(count.reshape(1, 1), *big, small, moments)
 
 
 def on_device(
@@ -394,9 +841,13 @@
     both = ("dp", "feat")
     row_lengths = lax.dynamic_index_in_dim(lengths, lax.axis_index("dp"), 0, keepdims=False)
     valid = (row_lengths[0] > 0).astype(f32)
-    features = lax.all_gather(feature_matrix, "feat", axis=1, tiled=True)
-    qkv = (mm("td,de->te", tokens, joint_weight) + joint_bias).astype(bf16)
-    attention, saved = attention_forward(qkv, features, valid, heads, size)
+    kernels = lax.axis_size("feat") == 4 and lax.axis_size("dp") == 8
+    if kernels:
+        attention, *saved = attention_call(tokens, joint_weight, joint_bias, feature_matrix, valid)
+    else:
+        features = lax.all_gather(feature_matrix, "feat", axis=1, tiled=True)
+        qkv = (mm("td,de->te", tokens, joint_weight) + joint_bias).astype(bf16)
+        attention, saved = attention_forward(qkv, features, valid, heads, size)
     branch_attn = mm("td,de->te", attention, output_weight) + output_bias
     wide = tokens.astype(f32)
     normal_1, inv_1 = layer_norm_parts(wide + branch_attn)
@@ -426,39 +877,49 @@
     g_first = layer_norm_back(g_hidden, normal_1, inv_1, first_gain)
     g_branch = g_first.astype(bf16)
     grad_outputbias = jnp.sum(g_branch.astype(f32), 0)
-    g_att = mm("te,de->td", g_branch, output_weight)
-    g_qkv = attention_backward(g_att, saved, features, valid, heads, size)
-    grad_jointbias = jnp.sum(g_qkv.astype(f32), 0)
-    input_gradient = g_first + mm("te,de->td", g_qkv, joint_weight)
-
     shards = lax.axis_size(both)
     each = model // shards
     widths = (3 * each, each, each, each, up_bias.shape[0] // shards, each, each, each, 3)
-    small = jnp.concatenate(
-        [
-            p.reshape(shards, -1)
-            for p in (
-                grad_jointbias,
-                grad_outputbias,
-                grad_firstgain,
-                grad_firstshift,
-                grad_upbias,
-                grad_downbias,
-                grad_secondgain,
-                grad_secondshift,
-            )
-        ]
-        + [jnp.broadcast_to(moments, (shards, 3))],
-        axis=1,
-    )
-    if lax.axis_size("feat") == 4 and lax.axis_size("dp") == 8 and sum(widths) <= 1024:
-        chips = shards // 2
-        packed = jnp.pad(small, ((0, 0), (0, 1024 - sum(widths)))).reshape(chips, 2, 8, 128)
-        *big, small = scatter_gradients(
-            chips, tokens, attention, hidden_low, activated, g_qkv, g_branch, g_pre, g_ffn, packed
+    row_sums = (
+        grad_outputbias,
+        grad_firstgain,
+        grad_firstshift,
+        grad_upbias,
+        grad_downbias,
+        grad_secondgain,
+        grad_secondshift,
+    )
+    count = jnp.sum(lengths).astype(f32) * model
+    if kernels:
+        *big, small, moment_sums, inputs = scatter_gradients(
+            shards // 2,
+            tokens,
+            attention,
+            hidden_low,
+            activated,
+            g_branch,
+            g_pre,
+            g_ffn,
+            saved,
+            (joint_weight, output_weight),
+            g_first,
+            [p.reshape(1, -1) for p in row_sums] + [jnp.pad(moments, (0, 125)).reshape(1, 128)],
         )
-        small = small.reshape(-1)
+        *big, input_gradient = big + [inputs]
+        *big, input_gradient, s0, s1, s2, s3, s4, s5, s6, s7, token_moments = finish(
+            count, [*big, input_gradient], small, moment_sums, widths
+        )
+        cuts = (s0, s1, s2, s3, s4, s5, s6, s7)
     else:
+        g_att = mm("te,de->td", g_branch, output_weight)
+        g_qkv = attention_backward(g_att, saved, features, valid, heads, size)
+        input_gradient = g_first + mm("te,de->td", g_qkv, joint_weight)
+        grad_jointbias = jnp.sum(g_qkv.astype(f32), 0)
+        small = jnp.concatenate(
+            [p.reshape(shards, -1) for p in (grad_jointbias, *row_sums)]
+            + [jnp.broadcast_to(moments, (shards, 3))],
+            axis=1,
+        )
         small = lax.psum_scatter(small, both, scatter_dimension=0, tiled=True)[0]
         pairs = (
             ("td,te->de", tokens, g_qkv),
@@ -472,13 +933,11 @@
             ).astype(f32)
             for spec, left, right in pairs
         ]
-    cuts, at = [], 0
-    for width in widths:
-        cuts.append(small[at : at + width])
-        at += width
-
-    valid_count = jnp.sum(lengths).astype(f32)
-    token_moments = jnp.sqrt(cuts[8] / (valid_count * model))
+        cuts, at = [], 0
+        for width in widths:
+            cuts.append(small[at : at + width])
+            at += width
+        token_moments = jnp.sqrt(cuts[8] / count)
     return (
         layer_output,
         input_gradient,

time: 251 us -> 152 us (0.61)
  blocking collectives: 58.6 us -> 0 us
  Pallas kernels: 78.7 us -> 119 us
  matrix products: 45.4 us -> 10.2 us
  local copies, waits for them, and re-layouts: 43.8 us -> 13 us
  other arithmetic: 20.5 us -> 6.95 us
    psum x2 -> x0, blocking collectives: 41 us -> none  [the longest x1 20.8 us: attention_backward(): g_state = lax.psum(mm('htm,htd->hmd', q_feat, g_num), 'feat').astype(bf16)]
    dot_general x17 -> x5, matrix products: 40 us -> 10.2 us  [mm(): return jnp.einsum(spec, a, b, preferred_element_type=f32)]
    pallas_call x0 -> x2, Pallas kernels: none -> 26 us  [the longest x1 23.3 us: attention_call(): pl.pallas_call(attention_kernel, out_shape=(jax.ShapeDtypeStruct((rows, m...]
    pallas_call x1, Pallas kernels: 78.7 us -> 93.1 us  [scatter_gradients(): pl.pallas_call(functools.partial(scatter_kernel, chips, model), out_shape...]
    reshape x12 -> x10, local copies, waits for them, and re-layouts: 18 us -> 6.05 us  [the longest x6 3.57 us: on_device(): p.reshape(1, -1)]
    slice x7 -> x0, local copies, waits for them, and re-layouts: 10.7 us -> none  [the longest x4 6.79 us: attention_forward(): qkv[:, i * model:(i + 1) * model].reshape(rows, heads, size)]
    all_gather x1 -> x0, blocking collectives: 10.3 us -> none  [on_device(): features = lax.all_gather(feature_matrix, 'feat', axis=1, tiled=True)]
    reduce_sum x7 -> x1, other arithmetic: 10.6 us -> 1.32 us  [on_device(): count = jnp.sum(lengths).astype(f32) * model]
where the time goes in v3:
time: 152 us
  Pallas kernels  119 us (78%)
  local copies, waits for them, and re-layouts  13 us (9%)
  matrix products  10.2 us (7%)
  other arithmetic  6.95 us (5%)
  between operations  2.48 us (2%)
    pallas_call x1, Pallas kernels, scatter_gradients(): pl.pallas_call(functools.partial(scatter_kernel, chips, model), out_shape...  93.1 us
    pallas_call x1, Pallas kernels, attention_call(): pl.pallas_call(attention_kernel, out_shape=(jax.ShapeDtypeStruct((rows, m...  23.3 us
    dot_general x5, matrix products, mm(): return jnp.einsum(spec, a, b, preferred_element_type=f32)  10.2 us
    unnamed x52, local copies, waits for them, and re-layouts  5.69 us
    reshape x6, local copies, waits for them, and re-layouts, on_device(): p.reshape(1, -1)  3.57 us

profile of v3, /device:TPU:0, one launch (start us, length us, event | category | flops | bytes accessed | tf_op | source)
XLA Modules:
  0.0 151.8 jit_solution(16243169845958963768)
XLA Ops:
  0.6 0.0 copy-start.22
  0.7 1.3 reduce_sum.175
  2.6 0.8 constant_dynamic-slice_fusion
  3.4 0.5 slice.4
  4.6 0.7 reshape.120.refs_2_
  5.3 1.1 copy.36
  6.4 0.1 reshape.122.refs_3_
  6.5 0.0 copy-start
  6.6 2.0 %copy-done = bf16[768,2304]{1,0:T(8,128)(2,1)S(1)} copy-done((bf16[768,2304]{1,0:T(8,128)(2,1)S(1)}, bf16[768,2304]{1,0:T(8,128)(2,1)}, u32[]{:S(2)}) %copy-start) | copy-done | bytes 3538968
  8.6 1.0 copy-done.3
  9.6 23.3 %attention.1 = (bf16[256,768]{1,0:T(8,128)(2,1)S(1)}, bf16[256,2304]{1,0:T(8,128)(2,1)S(1)}, bf16[256,3072]{1,0:T(8,128)(2,1)S(1)}, bf16[256,3072]{1,0:T(8,128)(...) custom-call(bf16[256,768]{1,0:T(8,128)(2,1)S(1)} %copy-done.3, ...), custom_call_target="tpu_custom_call" | custom-call | tf_op jit(solution)/shard_map/attention/pallas_call | solution.py:766
  32.9 0.0 copy-start.1
  32.9 0.0 copy-start.2
  32.9 0.0 copy-start.4
  32.9 0.0 copy-start.5
  32.9 0.0 copy-start.6
  32.9 0.0 copy-start.7
  32.9 0.0 copy-start.8
  32.9 0.0 copy-start.9
  32.9 0.0 copy-start.20
  33.0 0.0 copy-start.21
  33.0 1.2 fusion.15
  34.2 0.2 multiply_reduce_fusion.7
  34.4 0.0 slice-start
  34.4 0.2 fusion.10.refs_2_
  34.6 2.6 %copy-done.20 = bf16[768,3072]{1,0:T(8,128)(2,1)S(1)} copy-done((bf16[768,3072]{1,0:T(8,128)(2,1)S(1)}, bf16[768,3072]{1,0:T(8,128)(2,1)}, u32[]{:S(2)}) %copy-start.20) | copy-done | bytes 4718616
  37.2 2.1 %multiply_convert_fusion = (bf16[256,3072]{1,0:T(8,128)(2,1)S(1)}, f32[256,3072]{1,0:T(8,128)S(1)}) fusion(f32[3072]{0:T(1024)S(1)} %copy-done.21, bf16[256,768]{1,0:T(8,128)(2,1)S(1)} %fusion.10.refs_2_, bf16[768,3072]{1,0:T(8,128)(2,1)S(1)} %copy-done.20), kind=kOutput, calls=%fused_computation.9 | convolution fusion | flops 1212678144 | bytes 9842688 | tf_op jit(solution)/shard_map/td,df->tf/dot_general | solution.py:16
  39.5 0.0 copy-start.12
  39.5 0.0 copy-start.16
  39.5 0.0 copy-start.19
  39.5 2.1 %fusion.13 = (f32[256]{0:T(256)S(1)}, f32[256,768]{1,0:T(8,128)S(1)}, f32[]{:T(128)}) fusion(f32[768]{0:T(1024)S(1)} %copy-done.18, f32[768]{0:T(1024)S(1)} %copy-done.17, f32[256]{0:T(256)S(1)} %add_rsqrt_fusion.1, f32[256,768]{1,0:T(8,128)S(1)} %get-tuple-element.89, f32[256]{0:T(256)S(1)} %broadcast_multiply_fusion.5, f32[768]{0:T(1024)S(1)} %copy-done.23, ...), kind=kOutput, calls=%fused_computation.53 | convolution fusion | flops 1209728768 | bytes 7876612 | tf_op jit(solution)/shard_map/tf,fd->td/dot_general | solution.py:16
  41.6 2.0 %maximum_multiply_fusion = f32[3]{0:T(128)S(1)} fusion(f32[1]{0:T(128)} %bitcast.7, f32[1]{0:T(128)} %bitcast.6, f32[1]{0:T(128)} %bitcast.5, f32[]{:T(128)} %bitcast.2), kind=kLoop, calls=%fused_computation.43 | loop fusion | flops 9 | bytes 28 | tf_op jit(solution)/shard_map/mul | solution.py:863
  43.7 0.5 pad_bitcast_fusion.refs_24_
  44.2 0.2 multiply_reduce_fusion.6
  44.4 0.5 multiply_reduce_fusion.2
  44.9 0.6 reshape.129.refs_22_
  45.5 0.6 reshape.130.refs_23_
  46.1 1.2 convert_reduce_fusion.1
  47.2 2.9 %convert_reduce_fusion = (f32[3072]{0:T(1024)}, bf16[256,3072]{1,0:T(8,128)(2,1)S(1)}) fusion(f32[256,3072]{1,0:T(8,128)S(1)} %get-tuple-element.95, bf16[256,768]{1,0:T(8,128)(2,1)S(1)} %get-tuple-element.82.refs_6_, bf16[3072,768]{1,0:T(8,128)(2,1)S(1)} %bitcast.27), kind=kOutput, calls=%fused_computation.8 | convolution fusion | flops 1217393664 | bytes 9842688 | tf_op jit(solution)/shard_map/td,fd->tf/dot_general | solution.py:16
  50.2 0.0 copy-done.14
  50.2 0.6 reshape.128.refs_21_
  50.8 1.9 %multiply_reduce_fusion.3 = (f32[768]{0:T(1024)S(1)}, f32[256]{0:T(256)S(1)}, f32[256]{0:T(256)S(1)}, f32[768]{0:T(1024)S(1)}, f32[256,768]{1,0:T(8,128)S(1)}) fusion(f32[256,768]{1,0:T(8,128)S(1)} %get-tuple-element.89, f32[256]{0:T(256)S(1)} %add_rsqrt_fusion.1, f32[256]{0:T(256)S(1)} %broadcast_multiply_fusion.5, f32[768]{0:T(1024)S(1)} %copy-done.17, ...), kind=kOutput, calls=%fused_computation.21 | convolution fusion | flops 1211693056 | bytes 9064452 | tf_op jit(solution)/shard_map/tf,df->td/dot_general | solution.py:16
  52.7 0.6 reshape.125.refs_18_
  53.3 1.3 convert_reduce_fusion.2
  54.6 0.6 reshape.124.refs_17_
  55.2 0.6 reshape.126.refs_19_
  55.8 93.1 %scatter_gradients.1 = (f32[24,2304]{1,0:T(8,128)}, f32[24,768]{1,0:T(8,128)}, f32[24,3072]{1,0:T(8,128)}, f32[96,768]{1,0:T(8,128)}, f32[8,128]{1,0:T(8,128)}, /*index=5*/f32[8,128]{1,0:T(8,128)}, f32[256,768]{1,0:T(8,128)}) custom-call(bf16[256,768]{1,0:T(8,128)(2,1)} %refs_0_.3, bf16[256,768]{1,0:T(8,128)(2,1)} %copy-done.5, bf16[256,768]{1,0:T(8,128)(2,1)} %copy-done.13, ...), custom_call_target="tpu_custom_call" | custom-call | tf_op jit(solution)/shard_map/scatter_gradients/pallas_call | solution.py:566
  148.9 2.7 %finish.1 = (f32[24,2304]{1,0:T(8,128)}, f32[24,768]{1,0:T(8,128)}, f32[24,3072]{1,0:T(8,128)}, f32[96,768]{1,0:T(8,128)}, f32[256,768]{1,0:T(8,128)}, /*index=5...) custom-call(f32[1,1]{1,0:T(1,128)} %bitcast.3.refs_0_, ...), custom_call_target="tpu_custom_call" | custom-call | tf_op jit(solution)/shard_map/finish/pallas_call | solution.py:811
  (40 shorter events, 0.1 us)
Async XLA Ops:
  0.6 32.3 %copy-start.22 = (f32[768]{0:T(1024)S(1)}, f32[768]{0:T(1024)}, u32[]{:S(2)}) copy-start(f32[768]{0:T(1024)} %param.21) | copy-start | bytes 9220
  6.5 2.0 %copy-start = (bf16[768,2304]{1,0:T(8,128)(2,1)S(1)}, bf16[768,2304]{1,0:T(8,128)(2,1)}, u32[]{:S(2)}) copy-start(bf16[768,2304]{1,0:T(8,128)(2,1)} %refs_14_.1) | copy-start | bytes 10616836
  8.5 1.0 copy-start.3
  9.5 23.4 %copy-start.15 = (bf16[768,768]{1,0:T(8,128)(2,1)S(1)}, bf16[768,768]{1,0:T(8,128)(2,1)}, u32[]{:S(2)}) copy-start(bf16[768,768]{1,0:T(8,128)(2,1)} %refs_15_.1) | copy-start | bytes 3538948
  9.5 24.8 %copy-start.17 = (f32[768]{0:T(1024)S(1)}, f32[768]{0:T(1024)}, u32[]{:S(2)}) copy-start(f32[768]{0:T(1024)} %param.22) | copy-start | bytes 9220
  9.5 24.9 %copy-start.18 = (f32[768]{0:T(1024)S(1)}, f32[768]{0:T(1024)}, u32[]{:S(2)}) copy-start(f32[768]{0:T(1024)} %param.23) | copy-start | bytes 9220
  32.9 6.5 %copy-start.1 = (bf16[256,3072]{1,0:T(8,128)(2,1)}, bf16[256,3072]{1,0:T(8,128)(2,1)S(1)}, u32[]{:S(2)}) copy-start(bf16[256,3072]{1,0:T(8,128)(2,1)S(1)} %get-tuple-element.46.refs_8_) | copy-start | bytes 4718596
  32.9 6.5 %copy-start.2 = (bf16[256,3072]{1,0:T(8,128)(2,1)}, bf16[256,3072]{1,0:T(8,128)(2,1)S(1)}, u32[]{:S(2)}) copy-start(bf16[256,3072]{1,0:T(8,128)(2,1)S(1)} %get-tuple-element.47.refs_9_) | copy-start | bytes 4718596
  32.9 6.5 %copy-start.4 = (bf16[256,2304]{1,0:T(8,128)(2,1)}, bf16[256,2304]{1,0:T(8,128)(2,1)S(1)}, u32[]{:S(2)}) copy-start(bf16[256,2304]{1,0:T(8,128)(2,1)S(1)} %get-tuple-element.45.refs_7_) | copy-start | bytes 3538948
  32.9 6.5 %copy-start.5 = (bf16[256,768]{1,0:T(8,128)(2,1)}, bf16[256,768]{1,0:T(8,128)(2,1)S(1)}, u32[]{:S(2)}) copy-start(bf16[256,768]{1,0:T(8,128)(2,1)S(1)} %get-tuple-element.44.refs_1_) | copy-start | bytes 1179652
  32.9 6.5 %copy-start.6 = (bf16[6,128,256]{2,1,0:T(8,128)(2,1)}, bf16[6,128,256]{2,1,0:T(8,128)(2,1)S(1)}, u32[]{:S(2)}) copy-start(bf16[6,128,256]{2,1,0:T(8,128)(2,1)S(1)} %get-tuple-element.48.refs_10_) | copy-start | bytes 1179652
  32.9 6.5 %copy-start.7 = (bf16[6,256,128]{2,1,0:T(8,128)(2,1)}, bf16[6,256,128]{2,1,0:T(8,128)(2,1)S(1)}, u32[]{:S(2)}) copy-start(bf16[6,256,128]{2,1,0:T(8,128)(2,1)S(1)} %get-tuple-element.51.refs_13_) | copy-start | bytes 1179652
  32.9 6.5 %copy-start.8 = (f32[256,128]{1,0:T(8,128)}, f32[256,128]{1,0:T(8,128)S(1)}, u32[]{:S(2)}) copy-start(f32[256,128]{1,0:T(8,128)S(1)} %get-tuple-element.50.refs_12_) | copy-start | bytes 393220
  32.9 6.5 %copy-start.9 = (f32[16,256]{1,0:T(8,128)}, f32[16,256]{1,0:T(8,128)S(1)}, u32[]{:S(2)}) copy-start(f32[16,256]{1,0:T(8,128)S(1)} %get-tuple-element.49.refs_11_) | copy-start | bytes 49156
  32.9 4.3 %copy-start.20 = (bf16[768,3072]{1,0:T(8,128)(2,1)S(1)}, bf16[768,3072]{1,0:T(8,128)(2,1)}, u32[]{:S(2)}) copy-start(bf16[768,3072]{1,0:T(8,128)(2,1)} %param.24) | copy-start | bytes 14155780
  33.0 4.3 %copy-start.21 = (f32[3072]{0:T(1024)S(1)}, f32[3072]{0:T(1024)}, u32[]{:S(2)}) copy-start(f32[3072]{0:T(1024)} %param.25) | copy-start | bytes 36868
  34.4 5.0 %slice-start = ((s8[4718592]{0:T(1024)(128)(4,1)}), s8[4194304]{0:T(1024)(128)(4,1)S(1)}, s32[]{:S(2)}) async-start(s8[4718592]{0:T(1024)(128)(4,1)} %bitcast.26), calls=%async_computation | async-start | bytes 8388608
  37.2 2.2 %copy-start.13 = (bf16[256,768]{1,0:T(8,128)(2,1)}, bf16[256,768]{1,0:T(8,128)(2,1)S(1)}, u32[]{:S(2)}) copy-start(bf16[256,768]{1,0:T(8,128)(2,1)S(1)} %fusion.10.refs_2_) | copy-start | bytes 1179652
  37.2 2.2 %slice-start.1 = ((s8[4718592]{0:T(1024)(128)(4,1)}), s8[524288]{0:T(1024)(128)(4,1)S(1)}, s32[]{:S(2)}) async-start(s8[4718592]{0:T(1024)(128)(4,1)} %bitcast.26), calls=%async_computation.1 | async-start | bytes 1048576
  37.2 2.2 %copy-start.23 = (f32[768]{0:T(1024)S(1)}, f32[768]{0:T(1024)}, u32[]{:S(2)}) copy-start(f32[768]{0:T(1024)} %param.27) | copy-start | bytes 9220
  39.4 2.2 %copy-start.10 = (bf16[256,3072]{1,0:T(8,128)(2,1)}, bf16[256,3072]{1,0:T(8,128)(2,1)S(1)}, u32[]{:S(2)}) copy-start(bf16[256,3072]{1,0:T(8,128)(2,1)S(1)} %get-tuple-element.94.refs_3_) | copy-start | bytes 4718596
  39.5 4.9 %copy-start.12 = (bf16[256,768]{1,0:T(8,128)(2,1)S(1)}, bf16[256,768]{1,0:T(8,128)(2,1)}, u32[]{:S(2)}) copy-start(bf16[256,768]{1,0:T(8,128)(2,1)} %param.31) | copy-start | bytes 1179652
  39.5 4.9 %copy-start.16 = (f32[768]{0:T(1024)S(1)}, f32[768]{0:T(1024)}, u32[]{:S(2)}) copy-start(f32[768]{0:T(1024)} %param.28) | copy-start | bytes 9220
  39.5 6.6 %copy-start.19 = (f32[768]{0:T(1024)S(1)}, f32[768]{0:T(1024)}, u32[]{:S(2)}) copy-start(f32[768]{0:T(1024)} %param.29) | copy-start | bytes 9220
  47.2 2.9 %copy-start.14 = (bf16[256,768]{1,0:T(8,128)(2,1)}, bf16[256,768]{1,0:T(8,128)(2,1)S(1)}, u32[]{:S(2)}) copy-start(bf16[256,768]{1,0:T(8,128)(2,1)S(1)} %get-tuple-element.82.refs_6_) | copy-start | bytes 1179652
  50.2 2.5 %copy-start.11 = (bf16[256,3072]{1,0:T(8,128)(2,1)}, bf16[256,3072]{1,0:T(8,128)(2,1)S(1)}, u32[]{:S(2)}) copy-start(bf16[256,3072]{1,0:T(8,128)(2,1)S(1)} %get-tuple-element.98.refs_5_) | copy-start | bytes 4718596
